TPU v7x, 32 devices: a whole 2x2x4 slice. The times are simulated.
32 devices in a mesh: ctx: 16 (over z, y, core), tp: 2 (over x).
Axes of the slice: x: 2, y: 2, z: 4, core: 2. Of those that a mesh axis runs over, the one named last changes fastest.
Arguments:
- attn_q: bfloat16 [4096, 2048], P('ctx', 'tp'), may hold values from -5 to 5
- attn_k: bfloat16 [4096, 2048], P('ctx', 'tp'), may hold values from -5 to 5
- attn_v: bfloat16 [4096, 2048], P('ctx', 'tp'), may hold values from -6 to 6
- attn_o: bfloat16 [4096, 2048], P('ctx', 'tp'), may hold values from -6 to 6
- attn_dy: bfloat16 [4096, 8192], P('ctx', 'tp'), may hold values from -6 to 6
- out_weight: bfloat16 [2048, 8192], P('tp'), may hold values from -0.0625 to 0.0625
- block_place: int32 [32], replicated, may hold values from 0 to 31, each once
- hyena_q: bfloat16 [4096, 4096], P('ctx', 'tp'), may hold values from -6 to 6
- hyena_k: bfloat16 [4096, 4096], P('ctx', 'tp'), may hold values from -6 to 6
- hyena_v: bfloat16 [4096, 4096], P('ctx', 'tp'), may hold values from -6 to 6
- hyena_dy: bfloat16 [4096, 4096], P('ctx', 'tp'), may hold values from -6 to 6
- filter_residue: float32 [16, 32], P(None, 'tp')
- filter_rate: float32 [16, 32], P(None, 'tp'), as said below
Outputs:
- grad_q_attn: bfloat16 [4096, 2048], P('ctx', 'tp')
- grad_k_attn: bfloat16 [4096, 2048], P('ctx', 'tp')
- grad_v_attn: bfloat16 [4096, 2048], P('ctx', 'tp')
- grad_q_hyena: bfloat16 [4096, 4096], P('ctx', 'tp')
- grad_k_hyena: bfloat16 [4096, 4096], P('ctx', 'tp')
- grad_v_hyena: bfloat16 [4096, 4096], P('ctx', 'tp')
Inputs may be any that keep to these rules, and one draw needn't show every extreme that they name: A permutation of the 32 block places; index d of ctx holds, as its 256 rows of every attention array, the blocks at places block_place[2 d] and block_place[2 d + 1], in that order. `filter_rate`: positive, at most 1/30.
All inputs are finite; a program needn't handle non-finite values.
Results may differ from a plain program's by a relative error of at most 0.009.
Values may be sent and summed in bfloat16 or wider, within the bound.
A program may use at most 256 MiB of HBM per device.

v0:
```python
import functools
import math

import jax
import jax.numpy as jnp
from jax import lax
from jax.experimental import pallas as pl
from jax.experimental.pallas import tpu as pltpu
from jax.sharding import PartitionSpec as P

HD = 128
NEG_LARGE = -1e30
F32 = jnp.float32
BF16 = jnp.bfloat16
MESH = pl.DeviceIdType.MESH
LN2_SCALE = HD ** (-0.5) * math.log2(math.e)
SCALE = HD ** (-0.5)


def dot_nn(a, b):
    return lax.dot_general(a, b, (((1,), (0,)), ((), ())), preferred_element_type=F32)


def dot_nt(a, b):
    return lax.dot_general(a, b, (((1,), (1,)), ((), ())), preferred_element_type=F32)


def split(x):
    high = x.astype(BF16)
    return high, (x - high.astype(F32)).astype(BF16)


def rows_at(block, size):
    return pl.ds(pl.multiple_of(block * size, size), size)


def loop(start, stop, fn):
    def step(i, carry):
        fn(i)
        return carry

    lax.fori_loop(start, stop, step, 0)


class Plan:
    def __init__(self, count, parts, tok, feat, width, chan, modes, groups):
        self.count, self.parts = count, parts
        self.tok, self.feat, self.width = tok, feat, width
        self.chan, self.modes, self.groups = chan, modes, groups
        self.heads = feat // HD
        self.share = count // self.heads
        self.half = tok // 2
        self.near = 4 if count % 4 == 0 else count
        self.far = count // self.near
        self.chunks = 4
        self.piece = tok // self.chunks
        self.tile = min(256, feat)
        self.size = chan // groups
        self.blocks = max(
            sum(count - self.own(n, turn) for n in range(self.heads)) for turn in range(self.share)
        )

    def own(self, n, turn):
        return n * self.share + turn + (n % 2) * (self.share - 1 - 2 * turn)

    def offset(self, n, turn):
        share = self.share
        before = (
            share * (n * (n - 1) // 2) + ((n + 1) // 2) * turn + (n // 2) * (share - 1 - turn)
        )
        return n * self.count - before

    def held(self, i, turn):
        at = i // self.share
        mine = self.own(at, turn) - at * self.share
        return at + (i % self.share - mine + self.share) // self.share


def scratch(p):
    vm = pltpu.VMEM
    total = p.count * p.tok
    low = vm((total, HD), BF16)
    blocked = vm((2 * p.count, p.half, HD), BF16)
    other = max(p.share - 1, 1)
    rest = max(p.parts - 1, 1)
    lines = p.groups * p.modes
    dma = pltpu.SemaphoreType.DMA

    def pair(*shape):
        return [dma(shape), dma(shape)]

    items = dict(
        dy_own=vm((p.tok, p.width), BF16),
        dy_got=vm((rest, p.tok, p.width), BF16),
        w_own=vm((p.feat, p.width), BF16),
        w_rest=vm((rest, p.feat, p.width), BF16),
        g_part=vm((p.tok, p.feat), F32),
        o_buf=vm((p.tok, p.feat), BF16),
        g_low=vm((p.tok, p.feat), BF16),
        delta_out=vm((p.heads, 2, 8, HD), F32),
        delta_all=vm((2 * p.count, 8, HD), F32),
        delta_seq=vm((2 * p.count, 8, HD), F32),
        q_all=blocked,
        k_all=blocked,
        v_all=blocked,
        g_all=blocked,
        q_seq=low,
        k_seq=low,
        v_seq=low,
        g_seq=low,
        k_turn=vm((p.heads, HD, p.tok), BF16),
        cache=vm((p.blocks, p.tok, p.tok), BF16),
        ml=vm((p.heads * p.count, 8, p.tok), F32),
        ml_own=vm((p.count, 8, p.tok), F32),
        ml_got=vm((other, p.count, 8, p.tok), F32),
        dq_seq=vm((2 * p.count, p.half, HD), F32),
        dq_out=vm((other, 2 * p.heads, p.half, HD), F32),
        dq_got=vm((other, 2 * p.heads, p.half, HD), F32),
        dk_seq=blocked,
        dv_seq=blocked,
        send=vm((3, p.heads, 2, p.half, HD), BF16),
        hy_in=vm((4, p.tok, p.chan), BF16),
        hy_out=vm((3, p.tok, p.chan), BF16),
        st_own=vm((2, lines, HD), BF16),
        st_got=vm((p.near, 2, lines, HD), BF16),
        st_far=vm((2, lines, HD), BF16),
        far_got=vm((max(p.far - 1, 1), lines, HD), BF16),
        st_fin=vm((2, lines, HD), F32),
        sem_local=dma((16,)),
        sem_rest=dma((rest,)),
        sem_out=dma((6,)),
        sem_dy_s=dma((rest, p.chunks)),
        sem_dy_r=dma((rest, p.chunks)),
        sem_in_s=dma((3, p.heads)),
        sem_in_r=dma((3, p.heads)),
        sem_fw_s=dma((3, p.share)),
        sem_fw_r=dma((3, p.share)),
        sem_g_s=dma((p.chunks, p.heads)),
        sem_g_r=dma((p.chunks, p.heads)),
        sem_gf_s=dma((p.chunks, p.share)),
        sem_gf_r=dma((p.chunks, p.share)),
        sem_d_s=dma((p.heads,)),
        sem_d_r=dma((p.heads,)),
        sem_df_s=dma((p.share,)),
        sem_df_r=dma((p.share,)),
        sem_st_s=dma((p.near,)),
        sem_st_r=dma((p.near,)),
        sem_far_s=dma((p.far,)),
        sem_far_r=dma((p.far,)),
        sem_ml_s=dma((p.share,)),
        sem_ml_r=dma((p.share,)),
        sem_kv_s=dma((2, p.heads, p.share)),
        sem_kv_r=dma((2, p.heads, p.share)),
        sem_q_s=dma((p.share,)),
        sem_q_r=dma((p.share,)),
        sem_res_s=dma((3, p.heads)),
        sem_res_r=dma((3, p.heads)),
    )
    return items


class Refs:
    pass


INPUTS = (
    "table",
    "rate",
    "res",
    "attn_q",
    "attn_k",
    "attn_v",
    "attn_o",
    "attn_dy",
    "weight",
    "hy_q",
    "hy_k",
    "hy_v",
    "hy_dy",
)
OUTPUTS = ("out_q", "out_k", "out_v", "out_hq", "out_hk", "out_hv")


def column(ref, g):
    x = ref[...]
    lane = lax.broadcasted_iota(jnp.int32, x.shape, 1)
    return jnp.sum(jnp.where(lane == g, x, 0.0), axis=1, keepdims=True)


def kernel(p, names, *refs):
    r = Refs()
    for name, ref in zip(names, refs, strict=True):
        setattr(r, name, ref)
    me = lax.axis_index("ctx").astype(jnp.int32)
    at = lax.axis_index("tp").astype(jnp.int32)
    count, heads, share, tok, half = p.count, p.heads, p.share, p.tok, p.half
    head, turn = me // share, me % share

    def remote(src, dst, send, recv, ctx):
        return pltpu.make_async_remote_copy(
            src_ref=src,
            dst_ref=dst,
            send_sem=send,
            recv_sem=recv,
            device_id={"ctx": ctx},
            device_id_type=MESH,
        )

    def local(src, dst, sem):
        return pltpu.make_async_copy(src, dst, sem)

    def cols(h):
        return rows_at(h, HD)

    def pair_at(i):
        return pl.ds(2 * i, 2)

    barrier = pltpu.get_barrier_semaphore()
    for d in range(1, count):
        pl.semaphore_signal(
            barrier, inc=1, device_id={"ctx": (me + d) % count}, device_id_type=MESH
        )
    for d in range(1, p.parts):
        pl.semaphore_signal(
            barrier, inc=1, device_id={"tp": (at + d) % p.parts}, device_id_type=MESH
        )
    pl.semaphore_wait(barrier, count + p.parts - 2)

    def dy_copy(d, n):
        rows = pl.ds(n * p.piece, p.piece)
        return pltpu.make_async_remote_copy(
            src_ref=r.attn_dy.at[rows, :],
            dst_ref=r.dy_got.at[d - 1, rows, :],
            send_sem=r.sem_dy_s.at[d - 1, n],
            recv_sem=r.sem_dy_r.at[d - 1, n],
            device_id={"tp": (at + d) % p.parts},
            device_id_type=MESH,
        )

    for n in range(p.chunks):
        for d in range(1, p.parts):
            dy_copy(d, n).start()

    def part_cols(d):
        return rows_at((at - d + p.parts) % p.parts, p.width)

    hy_src = (r.hy_q, r.hy_k, r.hy_v, r.hy_dy)
    fetch_hy = [local(hy_src[i], r.hy_in.at[i], r.sem_local.at[i]) for i in range(4)]
    fetch_dy = local(r.attn_dy, r.dy_own, r.sem_local.at[4])
    fetch_w = local(r.weight.at[:, part_cols(0)], r.w_own, r.sem_local.at[5])
    fetch_o = local(r.attn_o, r.o_buf, r.sem_local.at[6])
    sources = (r.attn_k, r.attn_q, r.attn_v)
    alls = (r.k_all, r.q_all, r.v_all)
    seqs = (r.k_seq, r.q_seq, r.v_seq)
    own_slot = pair_at(turn * heads + head)
    fetch_own = [
        local(sources[i].at[:, :, cols(head)], alls[i].at[own_slot], r.sem_local.at[7 + i])
        for i in range(3)
    ]
    for c in fetch_hy:
        c.start()
    fetch_dy.start()
    fetch_w.start()

    def in_copy(i, d, arriving):
        to = (head + d) % heads
        source = (head - d + heads) % heads if arriving else head
        slot = pair_at(turn * heads + source)
        return remote(
            sources[i].at[:, :, cols(to)],
            alls[i].at[slot],
            r.sem_in_s.at[i, d],
            r.sem_in_r.at[i, d],
            to * share + turn,
        )

    for i in range(3):
        loop(1, heads, lambda d, i=i: in_copy(i, d, False).start())
    for c in fetch_own:
        c.start()
    fetch_o.start()
    fetch_rest = []
    for d in range(1, p.parts):
        c = local(r.weight.at[:, part_cols(d)], r.w_rest.at[d - 1], r.sem_rest.at[d - 1])
        fetch_rest.append(c)

    for c in fetch_hy:
        c.wait()
    lane_shape = (p.modes, tok)
    lag = lax.broadcasted_iota(jnp.int32, lane_shape, 1).astype(F32)

    def hy_block(i, g):
        return r.hy_in[i, :, rows_at(g, p.size)].astype(F32)

    def twice(x):
        return jnp.concatenate(split(x), axis=1)

    def state_of(decay, prod):
        both = dot_nn(jnp.concatenate(split(decay), axis=0), twice(prod))
        both = both[: p.modes] + both[p.modes :]
        return both[:, : p.size] + both[:, p.size :]

    def one_state(g):
        rate = column(r.rate, g)
        tail = jnp.exp(-rate * (tok - 1 - lag))
        first = jnp.exp(-rate * lag)
        lines = rows_at(g, p.modes)
        r.st_own[0, lines, :] = state_of(tail, hy_block(1, g) * hy_block(2, g)).astype(BF16)
        r.st_own[1, lines, :] = state_of(first, hy_block(0, g) * hy_block(3, g)).astype(BF16)

    loop(0, p.groups, one_state)

    near, far = p.near, p.far
    my_near, my_far = me % near, me // near

    def near_copy(d, arriving):
        source = (my_near - d + near) % near if arriving else my_near
        return remote(
            r.st_own,
            r.st_got.at[source],
            r.sem_st_s.at[d],
            r.sem_st_r.at[d],
            my_far * near + (my_near + d) % near,
        )

    loop(1, near, lambda d: near_copy(d, False).start())

    fetch_dy.wait()
    fetch_w.wait()
    for c in fetch_rest:
        c.start()

    def own_product(n):
        at_cols = rows_at(n, p.tile)
        r.g_part[:, at_cols] = dot_nt(r.dy_own[...], r.w_own[at_cols, :])

    loop(0, p.feat // p.tile, own_product)

    loop(1, near, lambda d: near_copy(d, True).wait_recv())
    r.st_got[my_near] = r.st_own[...]

    def decay(rate, steps, good):
        power = jnp.exp(-rate * (tok * jnp.maximum(steps, 0)).astype(F32))
        return jnp.where(good, power, 0.0)

    def near_sum(g):
        rate = column(r.rate, g)
        lines = rows_at(g, p.modes)
        zero = jnp.zeros((p.modes, p.size), F32)
        total, back, fin, fin_back = zero, zero, zero, zero
        for other in range(near):
            ahead = r.st_got[other, 0, lines, :].astype(F32)
            behind = r.st_got[other, 1, lines, :].astype(F32)
            total = total + decay(rate, jnp.int32(near - 1 - other), True) * ahead
            back = back + decay(rate, jnp.int32(other), True) * behind
            gap = my_near - 1 - other
            fin = fin + decay(rate, gap, gap >= 0) * ahead
            gap = other - 1 - my_near
            fin_back = fin_back + decay(rate, gap, gap >= 0) * behind
        r.st_far[0, lines, :] = total.astype(BF16)
        r.st_far[1, lines, :] = back.astype(BF16)
        r.st_fin[0, lines, :] = fin
        r.st_fin[1, lines, :] = fin_back

    loop(0, p.groups, near_sum)

    def far_copy(d):
        to = (my_far + d) % far
        return remote(
            r.st_far.at[(my_far + d) // far],
            r.far_got.at[d - 1],
            r.sem_far_s.at[d],
            r.sem_far_r.at[d],
            to * near + my_near,
        )

    loop(1, far, lambda d: far_copy(d).start())

    def hand_on(ref, i, s, arriving, sems):
        source = (turn - s + share) % share if arriving else turn
        part = pl.ds(source * heads * 2, heads * 2)
        return remote(
            ref.at[part],
            ref.at[part],
            sems[0].at[i, s],
            sems[1].at[i, s],
            head * share + (turn + s) % share,
        )

    fw = (r.sem_fw_s, r.sem_fw_r)

    def arrive(i):
        loop(1, heads, lambda d: in_copy(i, d, True).wait_recv())
        fetch_own[i].wait()
        for s in range(1, share):
            hand_on(alls[i], i, s, False, fw).start()

    def in_order(source, target):
        def one(place):
            target[rows_at(place, half), :] = source[r.table[0, place]]

        loop(0, 2 * count, one)

    def settle(i):
        for s in range(1, share):
            hand_on(alls[i], i, s, True, fw).wait_recv()
        in_order(alls[i], seqs[i])

    arrive(0)
    arrive(1)
    settle(0)
    settle(1)

    def g_place(n, source):
        slot, start = divmod(n * p.piece, half)
        return 2 * (turn * heads + source) + slot, pl.ds(start, p.piece)

    def g_copy(n, d, arriving):
        to = (head + d) % heads
        source = (head - d + heads) % heads if arriving else head
        rows = pl.ds(n * p.piece, p.piece)
        slot, inner = g_place(n, source)
        return remote(
            r.g_low.at[rows, cols(to)],
            r.g_all.at[slot, inner, :],
            r.sem_g_s.at[n, d],
            r.sem_g_r.at[n, d],
            to * share + turn,
        )

    def g_chunk(n):
        for d in range(1, p.parts):
            dy_copy(d, n).wait_recv()
        rows = pl.ds(n * p.piece, p.piece)

        def tile(c):
            at_cols = rows_at(c, p.tile)
            total = r.g_part[rows, at_cols]
            for d in range(1, p.parts):
                total = total + dot_nt(r.dy_got[d - 1, rows, :], r.w_rest[d - 1, at_cols, :])
            r.g_low[rows, at_cols] = total.astype(BF16)

        loop(0, p.feat // p.tile, tile)
        loop(1, heads, lambda d: g_copy(n, d, False).start())
        slot, inner = g_place(n, head)
        r.g_all[slot, inner, :] = r.g_low[rows, cols(head)]

    def g_arrive(n):
        loop(1, heads, lambda d: g_copy(n, d, True).wait_recv())

    for c in fetch_rest:
        c.wait()
    g_chunk(0)
    g_chunk(1)

    square = (tok, tok)
    row_id = lax.broadcasted_iota(jnp.int32, (8, tok), 0)
    empty = jnp.where(row_id == 0, NEG_LARGE, 0.0)

    def clear(n):
        r.ml[n] = empty

    loop(0, heads * count, clear)

    def turn_keys(n):
        mine = p.own(n, turn)
        r.k_turn[n] = r.k_seq[rows_at(mine, tok), :].astype(F32).T.astype(BF16)

    loop(0, heads, turn_keys)

    def spread(n):
        mine = p.own(n, turn)
        first = p.offset(n, turn)
        keys = rows_at(mine, tok)

        def one(i, masked=False):
            s = dot_nt(r.k_seq[keys, :], r.q_seq[rows_at(i, tok), :])
            if masked:
                key_id = lax.broadcasted_iota(jnp.int32, square, 0)
                query_id = lax.broadcasted_iota(jnp.int32, square, 1)
                s = jnp.where(key_id <= query_id, s, NEG_LARGE)
            peak = jnp.max(s, axis=0, keepdims=True)
            e = jnp.exp2((s - peak) * LN2_SCALE)
            r.cache[first + i - mine] = e.astype(BF16)
            r.ml[n * count + i, 0:1, :] = peak
            r.ml[n * count + i, 1:2, :] = jnp.sum(e, axis=0, keepdims=True)

        one(mine, True)
        loop(mine + 1, count, one)

    loop(0, heads, spread)

    def combine(i):
        peaks = [r.ml[n * count + i, 0:1, :] for n in range(heads)]
        peak = functools.reduce(jnp.maximum, peaks)
        total = 0.0
        for n in range(heads):
            weight = jnp.exp2((peaks[n] - peak) * LN2_SCALE)
            total = total + weight * r.ml[n * count + i, 1:2, :]
        r.ml_own[i, 0:1, :] = peak
        r.ml_own[i, 1:2, :] = total

    def clear_own(i):
        r.ml_own[i] = empty

    loop(0, count, clear_own)
    loop(0, count, combine)

    def ml_copy(s):
        return remote(
            r.ml_own,
            r.ml_got.at[s - 1],
            r.sem_ml_s.at[s],
            r.sem_ml_r.at[s],
            head * share + (turn + s) % share,
        )

    for s in range(1, share):
        ml_copy(s).start()
    arrive(2)
    g_chunk(2)
    for s in range(1, share):
        ml_copy(s).wait_recv()
        ml_copy(s).wait_send()

    def join(i):
        peaks = [r.ml_own[i, 0:1, :]] + [r.ml_got[s, i, 0:1, :] for s in range(share - 1)]
        peak = functools.reduce(jnp.maximum, peaks)
        total = jnp.exp2((peaks[0] - peak) * LN2_SCALE) * r.ml_own[i, 1:2, :]
        for s in range(share - 1):
            weight = jnp.exp2((peaks[s + 1] - peak) * LN2_SCALE)
            total = total + weight * r.ml_got[s, i, 1:2, :]
        r.ml_own[i, 0:1, :] = peak
        r.ml_own[i, 1:2, :] = 1.0 / total

    loop(0, count, join)

    def normal(n):
        mine = p.own(n, turn)
        first = p.offset(n, turn)

        def one(i):
            weight = jnp.exp2((r.ml[n * count + i, 0:1, :] - r.ml_own[i, 0:1, :]) * LN2_SCALE)
            weight = weight * r.ml_own[i, 1:2, :]
            e = r.cache[first + i - mine].astype(F32)
            r.cache[first + i - mine] = (e * weight).astype(BF16)

        loop(mine, count, one)

    loop(0, heads, normal)
    settle(2)

    loop(1, far, lambda d: far_copy(d).wait_recv())

    def far_sum(g):
        rate = column(r.rate, g)
        lines = rows_at(g, p.modes)
        ahead = jnp.zeros((p.modes, p.size), F32)
        behind = ahead
        for d in range(1, far):
            got = r.far_got[d - 1, lines, :].astype(F32)
            source = (my_far - d + far) % far
            gap = (my_far - 1 - source) * near + my_near
            ahead = ahead + decay(rate, gap, source < my_far) * got
            gap = (source - 1 - my_far) * near + near - 1 - my_near
            behind = behind + decay(rate, gap, source > my_far) * got
        r.st_fin[0, lines, :] += ahead
        r.st_fin[1, lines, :] += behind

    loop(0, p.groups, far_sum)

    gf = (r.sem_gf_s, r.sem_gf_r)

    def g_hand(n, s, arriving):
        source = (turn - s + share) % share if arriving else turn
        part = pl.ds(source * heads * 2, heads * 2)
        return remote(
            r.g_all.at[part],
            r.g_all.at[part],
            gf[0].at[n, s],
            gf[1].at[n, s],
            head * share + (turn + s) % share,
        )

    for n in range(3, p.chunks):
        g_chunk(n)
    fetch_o.wait()
    ones = jnp.ones((8, HD), BF16)

    def delta_of(h):
        prod = r.g_low[:, cols(h)].astype(F32) * r.o_buf[:, cols(h)].astype(F32)
        high, low = split(prod)
        value = dot_nt(ones, high) + dot_nt(ones, low)
        r.delta_out[h, 0] = value[:, :half]
        r.delta_out[h, 1] = value[:, half:]

    loop(0, heads, delta_of)

    def delta_copy(d, arriving):
        to = (head + d) % heads
        source = (head - d + heads) % heads if arriving else head
        return remote(
            r.delta_out.at[to],
            r.delta_all.at[pl.ds((turn * heads + source) * 2, 2)],
            r.sem_d_s.at[d],
            r.sem_d_r.at[d],
            to * share + turn,
        )

    loop(1, heads, lambda d: delta_copy(d, False).start())
    r.delta_all[pl.ds((turn * heads + head) * 2, 2)] = r.delta_out[head]

    def delta_hand(s, arriving):
        source = (turn - s + share) % share if arriving else turn
        part = pl.ds(source * heads * 2, heads * 2)
        return remote(
            r.delta_all.at[part],
            r.delta_all.at[part],
            r.sem_df_s.at[s],
            r.sem_df_r.at[s],
            head * share + (turn + s) % share,
        )

    for n in range(p.chunks):
        g_arrive(n)
    for s in range(1, share):
        g_hand(0, s, False).start()
    loop(1, heads, lambda d: delta_copy(d, True).wait_recv())
    for s in range(1, share):
        delta_hand(s, False).start()
    for s in range(1, share):
        g_hand(0, s, True).wait_recv()
        delta_hand(s, True).wait_recv()
    in_order(r.g_all, r.g_seq)

    def order_delta(place):
        r.delta_seq[place] = r.delta_all[r.table[0, place]]

    loop(0, 2 * count, order_delta)

    def column_pass(kind, other, target, factor):
        def one(n):
            mine = p.own(n, turn)
            first = p.offset(n, turn)

            def add(i, acc):
                return acc + dot_nn(r.cache[first + i - mine], other[rows_at(i, tok), :])

            acc = lax.fori_loop(mine, count, add, jnp.zeros((tok, HD), F32))
            value = (acc * factor).astype(BF16)
            target[2 * mine] = value[:half]
            target[2 * mine + 1] = value[half:]
            for s in range(1, share):
                kv_copy(kind, n, s, target, False).start()

        loop(0, heads, one)

    def kv_copy(kind, n, s, target, arriving):
        source = (turn - s + share) % share if arriving else turn
        rows = pair_at(p.own(n, source))
        return remote(
            target.at[rows],
            target.at[rows],
            r.sem_kv_s.at[kind, n, s],
            r.sem_kv_r.at[kind, n, s],
            head * share + (turn + s) % share,
        )

    def kv_arrive(kind, target):
        def one(n):
            for s in range(1, share):
                kv_copy(kind, n, s, target, True).wait_recv()

        loop(0, heads, one)

    outs = (r.out_q, r.out_k, r.out_v)

    def res_copy(kind, d):
        to = (head + d) % heads
        return remote(
            r.send.at[kind, d],
            outs[kind].at[:, :, cols(head)],
            r.sem_res_s.at[kind, d],
            r.sem_res_r.at[kind, d],
            to * share + turn,
        )

    def res_local(kind):
        return local(r.send.at[kind, 0], outs[kind].at[:, :, cols(head)], r.sem_out.at[kind])

    def hand_back(kind, value_of):
        def one(d):
            flat = (turn * heads + (head + d) % heads) * 2
            for b in range(2):
                place = r.table[1, flat + b]
                value = value_of(place, (head + d) % heads, b)
                r.send[kind, d, b] = value

        def both(d):
            one(d)
            res_copy(kind, d).start()

        loop(1, heads, both)
        one(0)
        res_local(kind).start()

    column_pass(0, r.g_seq, r.dv_seq, 1.0)
    kv_arrive(0, r.dv_seq)
    hand_back(2, lambda place, h, b: r.dv_seq[place])

    def row_pass(i):
        g = r.g_seq[rows_at(i, tok), :]
        delta = jnp.concatenate(
            [r.delta_seq[2 * i, 0:1, :], r.delta_seq[2 * i + 1, 0:1, :]], axis=1
        )

        def one(n, acc):
            mine = p.own(n, turn)
            where = p.offset(n, turn) + i - mine
            grad_prob = dot_nt(r.v_seq[rows_at(mine, tok), :], g)
            grad_score = (r.cache[where].astype(F32) * (grad_prob - delta)).astype(BF16)
            r.cache[where] = grad_score
            return acc + dot_nn(r.k_turn[n], grad_score)

        acc = lax.fori_loop(0, p.held(i, turn), one, jnp.zeros((HD, tok), F32))
        value = acc.T * SCALE
        r.dq_seq[2 * i] = value[:half]
        r.dq_seq[2 * i + 1] = value[half:]

    loop(0, count, row_pass)

    def q_copy(s):
        return remote(
            r.dq_out.at[s - 1],
            r.dq_got.at[s - 1],
            r.sem_q_s.at[s],
            r.sem_q_r.at[s],
            head * share + (turn + s) % share,
        )

    for s in range(1, share):

        def pick(f, s=s):
            place = r.table[1, (turn + s) % share * heads * 2 + f]
            r.dq_out[s - 1, f] = r.dq_seq[place]

        loop(0, 2 * heads, pick)
        q_copy(s).start()

    column_pass(1, r.q_seq, r.dk_seq, SCALE)
    for s in range(1, share):
        q_copy(s).wait_recv()

    def dq_value(place, h, b):
        value = r.dq_seq[place]
        for s in range(1, share):
            value = value + r.dq_got[s - 1, 2 * h + b]
        return value.astype(BF16)

    hand_back(0, dq_value)
    kv_arrive(1, r.dk_seq)
    hand_back(1, lambda place, h, b: r.dk_seq[place])

    lag_id = lax.broadcasted_iota(jnp.int32, lane_shape, 1)
    turned = jnp.where(lag_id == 0, 0, tok - lag_id).astype(F32)
    tall = (half, tok)
    row = lax.broadcasted_iota(jnp.int32, (half, half), 0)
    col = lax.broadcasted_iota(jnp.int32, (half, half), 1)
    blank = jnp.zeros((half, half), F32)

    def mixed(bands, prod, edge, state):
        high, low = split(bands)
        pair = twice(prod)
        out = dot_nn(high, pair) + dot_nn(low, pair)
        e_high = edge.astype(BF16).astype(F32)
        s_high, s_low = split(state)
        left = jnp.concatenate([e_high, edge - e_high, e_high], axis=0).T.astype(BF16)
        right = jnp.concatenate([s_high, s_high, s_low], axis=0)
        return out[:, : p.size] + out[:, p.size :] + dot_nn(left, right)

    def mix(g):
        rate = jnp.broadcast_to(column(r.rate, g), lane_shape)
        res = jnp.broadcast_to(column(r.res, g), lane_shape)
        taps = jnp.sum(res * jnp.exp(-rate * lag), axis=0, keepdims=True)
        back_taps = jnp.sum(res * jnp.exp(-rate * turned), axis=0, keepdims=True)
        lower = pltpu.roll(jnp.broadcast_to(back_taps, tall), 0, 1, stride=1, stride_axis=0)
        upper = pltpu.roll(jnp.broadcast_to(taps, tall), 0, 1, stride=1, stride_axis=0)
        near_low = jnp.where(col <= row, lower[:, :half], 0.0)
        near_up = jnp.where(col >= row, upper[:, :half], 0.0)
        lower = jnp.concatenate(
            [
                jnp.concatenate([near_low, blank], axis=1),
                jnp.concatenate([lower[:, half:], near_low], axis=1),
            ],
            axis=0,
        )
        upper = jnp.concatenate(
            [
                jnp.concatenate([near_up, upper[:, half:]], axis=1),
                jnp.concatenate([blank, near_up], axis=1),
            ],
            axis=0,
        )
        lines = rows_at(g, p.modes)
        into = res * jnp.exp(-rate * (lag + 1.0))
        back = res * jnp.exp(-rate * (tok - lag))
        k, v, dy = hy_block(1, g), hy_block(2, g), hy_block(3, g)
        conv = mixed(lower, k * v, into, r.st_fin[0, lines, :])
        mid = mixed(upper, hy_block(0, g) * dy, back, r.st_fin[1, lines, :])
        here = rows_at(g, p.size)
        r.hy_out[0, :, here] = (dy * conv).astype(BF16)
        r.hy_out[1, :, here] = (mid * v).astype(BF16)
        r.hy_out[2, :, here] = (mid * k).astype(BF16)

    loop(0, p.groups, mix)
    hy_outs = (r.out_hq, r.out_hk, r.out_hv)
    give = [local(r.hy_out.at[i], hy_outs[i], r.sem_out.at[3 + i]) for i in range(3)]
    for c in give:
        c.start()

    for n in range(p.chunks):
        for d in range(1, p.parts):
            dy_copy(d, n).wait_send()
    loop(1, near, lambda d: near_copy(d, False).wait_send())
    loop(1, far, lambda d: far_copy(d).wait_send())
    for i in range(3):
        loop(1, heads, lambda d, i=i: in_copy(i, d, False).wait_send())
        for s in range(1, share):
            hand_on(alls[i], i, s, False, fw).wait_send()
    for n in range(p.chunks):
        loop(1, heads, lambda d, n=n: g_copy(n, d, False).wait_send())
    loop(1, heads, lambda d: delta_copy(d, False).wait_send())
    for s in range(1, share):
        g_hand(0, s, False).wait_send()
        delta_hand(s, False).wait_send()
        q_copy(s).wait_send()

        def kv_sent(n, s=s):
            kv_copy(0, n, s, r.dv_seq, False).wait_send()
            kv_copy(1, n, s, r.dk_seq, False).wait_send()

        loop(0, heads, kv_sent)
    for kind in range(3):
        loop(1, heads, lambda d, kind=kind: res_copy(kind, d).wait_send())
        loop(1, heads, lambda d, kind=kind: res_copy(kind, d).wait_recv())
        res_local(kind).wait()
    for c in give:
        c.wait()


def body(
    attn_q,
    attn_k,
    attn_v,
    attn_o,
    attn_dy,
    out_weight,
    block_place,
    hyena_q,
    hyena_k,
    hyena_v,
    hyena_dy,
    filter_residue,
    filter_rate,
):
    tok, feat = attn_q.shape
    chan = hyena_q.shape[1]
    modes, groups = filter_rate.shape
    count, parts = lax.axis_size("ctx"), lax.axis_size("tp")
    p = Plan(count, parts, tok, feat, attn_dy.shape[1], chan, modes, groups)
    places = block_place.reshape(p.heads, p.share, 2).transpose(1, 0, 2).reshape(-1)
    slot = jnp.arange(2 * count, dtype=jnp.int32)
    found = jnp.where(places[None, :] == slot[:, None], slot[None, :], 0)
    table = jnp.stack([jnp.sum(found, axis=1), places])
    items = scratch(p)
    names = INPUTS + OUTPUTS + tuple(items)
    hbm = pl.BlockSpec(memory_space=pl.ANY)
    vmem = pl.BlockSpec(memory_space=pltpu.VMEM)
    attn_out = jax.ShapeDtypeStruct((2, p.half, feat), BF16)
    hy_out = jax.ShapeDtypeStruct((tok, chan), BF16)
    outs = pl.pallas_call(
        functools.partial(kernel, p, names),
        in_specs=[pl.BlockSpec(memory_space=pltpu.SMEM), vmem, vmem] + [hbm] * 10,
        out_specs=[hbm] * 6,
        out_shape=[attn_out] * 3 + [hy_out] * 3,
        scratch_shapes=list(items.values()),
        compiler_params=pltpu.CompilerParams(
            collective_id=0, has_side_effects=True, vmem_limit_bytes=63 * 1024 * 1024
        ),
        name="grads",
    )(
        table,
        filter_rate,
        filter_residue,
        attn_q.reshape(2, p.half, feat),
        attn_k.reshape(2, p.half, feat),
        attn_v.reshape(2, p.half, feat),
        attn_o,
        attn_dy,
        out_weight,
        hyena_q,
        hyena_k,
        hyena_v,
        hyena_dy,
    )
    return tuple(x.reshape(tok, feat) for x in outs[:3]) + tuple(outs[3:])


def solution(mesh):
    both = P("ctx", "tp")
    in_specs = (both,) * 5 + (P("tp", None), P()) + (both,) * 4 + (P(None, "tp"),) * 2
    return jax.shard_map(body, mesh=mesh, in_specs=in_specs, out_specs=(both,) * 6, check_vma=False)
```

profile of v0, /device:TPU:13, one launch (start us, length us, event | category | flops | bytes accessed | tf_op | source)
XLA Modules:
  0.0 179.4 jit_solution(3888059375840794169)
XLA Ops:
  0.6 0.7 reshape.34
  1.4 0.1 broadcast_in_dim_reshape.3
  1.5 0.1 eq.15
  1.6 0.1 select_reduce_fusion
  1.7 0.6 pad_add_fusion.refs_0_
  2.3 164.6 %grads.1 = (bf16[2,128,1024]{2,1,0:T(8,128)(2,1)}, bf16[2,128,1024]{2,1,0:T(8,128)(2,1)}, bf16[2,128,1024]{2,1,0:T(8,128)(2,1)}, bf16[256,2048]{1,0:T(8,128)(2,1...) custom-call(s32[2,32]{1,0:T(2,128)} %pad_add_fusion.refs_0_, f32[16,16]{1,0:T(8,128)} %refs_1_.1, ...), custom_call_target="tpu_custom_call" | custom-call | tf_op jit(solution)/shard_map/grads/pallas_call | solution.py:881
  166.9 1.9 %copy.31 = bf16[256,1024]{1,0:T(8,128)(2,1)} copy(bf16[256,1024]{1,0:T(8,128)(2,1)} %bitcast.13) | data formatting | bytes 1048576
  168.8 1.9 %copy.32 = bf16[256,1024]{1,0:T(8,128)(2,1)} copy(bf16[256,1024]{1,0:T(8,128)(2,1)} %bitcast.12) | data formatting | bytes 1048576
  170.6 1.9 %copy.33 = bf16[256,1024]{1,0:T(8,128)(2,1)} copy(bf16[256,1024]{1,0:T(8,128)(2,1)} %bitcast.11) | data formatting | bytes 1048576
  172.5 2.3 %copy.34 = bf16[256,2048]{1,0:T(8,128)(2,1)} copy(bf16[256,2048]{1,0:T(8,128)(2,1)} %get-tuple-element.27) | data formatting | bytes 2097152
  174.8 2.3 %copy.35 = bf16[256,2048]{1,0:T(8,128)(2,1)} copy(bf16[256,2048]{1,0:T(8,128)(2,1)} %get-tuple-element.28) | data formatting | bytes 2097152
  177.1 2.3 %copy.36 = bf16[256,2048]{1,0:T(8,128)(2,1)} copy(bf16[256,2048]{1,0:T(8,128)(2,1)} %get-tuple-element.29) | data formatting | bytes 2097152
  (1 shorter events, 0.0 us)
where the time goes:
time: 180 us; the launch traced here: 179 us
  Pallas kernels  165 us (92%)
  local copies, waits for them, and re-layouts  13.4 us (7%)
    pallas_call x1, Pallas kernels, body(): pl.pallas_call(functools.partial(kernel, p, names), in_specs=[pl.BlockSpe...  165 us
    unnamed x6, local copies, waits for them, and re-layouts  12.5 us

commit v1 on v0

--- a/solution.py
+++ b/solution.py
@@ -40,6 +40,16 @@
         return carry
 
     lax.fori_loop(start, stop, step, 0)
+
+
+def spans(start, stop, fn, carry=0):
+    for width in (4, 2, 1):
+        turns = (stop - start) // width
+        carry = lax.fori_loop(
+            0, turns, lambda t, c, s=start, w=width: fn(s + w * t, w, c), carry
+        )
+        start = start + width * turns
+    return carry
 
 
 class Plan:
@@ -97,9 +107,10 @@
         g_part=vm((p.tok, p.feat), F32),
         o_buf=vm((p.tok, p.feat), BF16),
         g_low=vm((p.tok, p.feat), BF16),
-        delta_out=vm((p.heads, 2, 8, HD), F32),
+        table=pltpu.SMEM((2, 2 * p.count), jnp.int32),
+        delta_out=vm((2, p.heads, 8, HD), F32),
         delta_all=vm((2 * p.count, 8, HD), F32),
-        delta_seq=vm((2 * p.count, 8, HD), F32),
+        delta_row=vm((p.count, 8, p.tok), F32),
         q_all=blocked,
         k_all=blocked,
         v_all=blocked,
@@ -113,6 +124,7 @@
         ml=vm((p.heads * p.count, 8, p.tok), F32),
         ml_own=vm((p.count, 8, p.tok), F32),
         ml_got=vm((other, p.count, 8, p.tok), F32),
+        dq_turn=vm((p.count, HD, p.tok), F32),
         dq_seq=vm((2 * p.count, p.half, HD), F32),
         dq_out=vm((other, 2 * p.heads, p.half, HD), F32),
         dq_got=vm((other, 2 * p.heads, p.half, HD), F32),
@@ -139,10 +151,10 @@
         sem_g_r=dma((p.chunks, p.heads)),
         sem_gf_s=dma((p.chunks, p.share)),
         sem_gf_r=dma((p.chunks, p.share)),
-        sem_d_s=dma((p.heads,)),
-        sem_d_r=dma((p.heads,)),
-        sem_df_s=dma((p.share,)),
-        sem_df_r=dma((p.share,)),
+        sem_d_s=dma((2, p.heads)),
+        sem_d_r=dma((2, p.heads)),
+        sem_df_s=dma((2, p.share)),
+        sem_df_r=dma((2, p.share)),
         sem_st_s=dma((p.near,)),
         sem_st_r=dma((p.near,)),
         sem_far_s=dma((p.far,)),
@@ -164,7 +176,7 @@
 
 
 INPUTS = (
-    "table",
+    "places",
     "rate",
     "res",
     "attn_q",
@@ -274,7 +286,7 @@
             to * share + turn,
         )
 
-    for i in range(3):
+    for i in range(2):
         loop(1, heads, lambda d, i=i: in_copy(i, d, False).start())
     for c in fetch_own:
         c.start()
@@ -376,6 +388,33 @@
 
     loop(1, far, lambda d: far_copy(d).start())
 
+    def place_of(flat):
+        source, h = flat // (2 * heads), flat // 2 % heads
+        return r.places[(h * share + source) * 2 + flat % 2]
+
+    def find(place):
+        slot = jnp.int32(0)
+        for stored in range(2 * count):
+            c, b = divmod(stored, 2)
+            flat = c % share * heads + c // share
+            slot = jnp.where(r.places[stored] == place, 2 * flat + b, slot)
+        r.table[0, place] = slot
+        r.table[1, place] = slot % 2 * count + slot // 2
+
+    loop(0, 2 * count, find)
+
+    def clear_queries(i):
+        r.dq_turn[i] = jnp.zeros((HD, tok), F32)
+
+    loop(0, count, clear_queries)
+    row_id = lax.broadcasted_iota(jnp.int32, (8, tok), 0)
+    empty = jnp.where(row_id == 0, NEG_LARGE, 0.0)
+
+    def clear(n):
+        r.ml[n] = empty
+
+    loop(0, heads * count, clear)
+
     def hand_on(ref, i, s, arriving, sems):
         source = (turn - s + share) % share if arriving else turn
         part = pl.ds(source * heads * 2, heads * 2)
@@ -395,25 +434,20 @@
         for s in range(1, share):
             hand_on(alls[i], i, s, False, fw).start()
 
-    def in_order(source, target):
+    def in_order(source, target, row):
         def one(place):
-            target[rows_at(place, half), :] = source[r.table[0, place]]
+            target[rows_at(place, half), :] = source[r.table[row, place]]
 
         loop(0, 2 * count, one)
 
     def settle(i):
         for s in range(1, share):
             hand_on(alls[i], i, s, True, fw).wait_recv()
-        in_order(alls[i], seqs[i])
-
-    arrive(0)
-    arrive(1)
-    settle(0)
-    settle(1)
+        in_order(alls[i], seqs[i], 0)
 
     def g_place(n, source):
         slot, start = divmod(n * p.piece, half)
-        return 2 * (turn * heads + source) + slot, pl.ds(start, p.piece)
+        return slot * count + turn * heads + source, pl.ds(start, p.piece)
 
     def g_copy(n, d, arriving):
         to = (head + d) % heads
@@ -435,38 +469,81 @@
 
         def tile(c):
             at_cols = rows_at(c, p.tile)
-            total = r.g_part[rows, at_cols]
-            for d in range(1, p.parts):
-                total = total + dot_nt(r.dy_got[d - 1, rows, :], r.w_rest[d - 1, at_cols, :])
-            r.g_low[rows, at_cols] = total.astype(BF16)
+            total = dot_nt(r.w_rest[0, at_cols, :], r.dy_got[0, rows, :])
+            for d in range(2, p.parts):
+                total = total + dot_nt(r.w_rest[d - 1, at_cols, :], r.dy_got[d - 1, rows, :])
+            r.g_low[rows, at_cols] = (r.g_part[rows, at_cols] + total.T).astype(BF16)
 
         loop(0, p.feat // p.tile, tile)
         loop(1, heads, lambda d: g_copy(n, d, False).start())
         slot, inner = g_place(n, head)
         r.g_all[slot, inner, :] = r.g_low[rows, cols(head)]
 
+    def g_hand(n, s, arriving):
+        source = (turn - s + share) % share if arriving else turn
+        slot, start = divmod(n * p.piece, half)
+        part = r.g_all.at[
+            pl.ds(slot * count + source * heads, heads), pl.ds(start, p.piece), :
+        ]
+        return remote(
+            part,
+            part,
+            r.sem_gf_s.at[n, s],
+            r.sem_gf_r.at[n, s],
+            head * share + (turn + s) % share,
+        )
+
     def g_arrive(n):
         loop(1, heads, lambda d: g_copy(n, d, True).wait_recv())
-
-    for c in fetch_rest:
-        c.wait()
-    g_chunk(0)
-    g_chunk(1)
+        for s in range(1, share):
+            g_hand(n, s, False).start()
+
+    ones = jnp.ones((8, HD), BF16)
+
+    def delta_copy(b, d, arriving):
+        to = (head + d) % heads
+        source = (head - d + heads) % heads if arriving else head
+        return remote(
+            r.delta_out.at[b, to],
+            r.delta_all.at[b * count + turn * heads + source],
+            r.sem_d_s.at[b, d],
+            r.sem_d_r.at[b, d],
+            to * share + turn,
+        )
+
+    def delta_half(b):
+        rows = pl.ds(b * half, half)
+
+        def one(h):
+            prod = r.g_low[rows, cols(h)].astype(F32) * r.o_buf[rows, cols(h)].astype(F32)
+            high, low = split(prod)
+            r.delta_out[b, h] = dot_nt(ones, high) + dot_nt(ones, low)
+
+        loop(0, heads, one)
+        loop(1, heads, lambda d: delta_copy(b, d, False).start())
+        r.delta_all[b * count + turn * heads + head] = r.delta_out[b, head]
+
+    def delta_hand(b, s, arriving):
+        source = (turn - s + share) % share if arriving else turn
+        part = r.delta_all.at[pl.ds(b * count + source * heads, heads)]
+        return remote(
+            part,
+            part,
+            r.sem_df_s.at[b, s],
+            r.sem_df_r.at[b, s],
+            head * share + (turn + s) % share,
+        )
+
+    def delta_arrive(b):
+        loop(1, heads, lambda d: delta_copy(b, d, True).wait_recv())
+        for s in range(1, share):
+            delta_hand(b, s, False).start()
 
     square = (tok, tok)
-    row_id = lax.broadcasted_iota(jnp.int32, (8, tok), 0)
-    empty = jnp.where(row_id == 0, NEG_LARGE, 0.0)
-
-    def clear(n):
-        r.ml[n] = empty
-
-    loop(0, heads * count, clear)
 
     def turn_keys(n):
         mine = p.own(n, turn)
         r.k_turn[n] = r.k_seq[rows_at(mine, tok), :].astype(F32).T.astype(BF16)
-
-    loop(0, heads, turn_keys)
 
     def spread(n):
         mine = p.own(n, turn)
@@ -485,10 +562,13 @@
             r.ml[n * count + i, 0:1, :] = peak
             r.ml[n * count + i, 1:2, :] = jnp.sum(e, axis=0, keepdims=True)
 
+        def some(i, width, carry):
+            for u in range(width):
+                one(i + u)
+            return carry
+
         one(mine, True)
-        loop(mine + 1, count, one)
-
-    loop(0, heads, spread)
+        spans(mine + 1, count, some)
 
     def combine(i):
         peaks = [r.ml[n * count + i, 0:1, :] for n in range(heads)]
@@ -497,14 +577,9 @@
         for n in range(heads):
             weight = jnp.exp2((peaks[n] - peak) * LN2_SCALE)
             total = total + weight * r.ml[n * count + i, 1:2, :]
+        r.ml_own[i] = empty
         r.ml_own[i, 0:1, :] = peak
         r.ml_own[i, 1:2, :] = total
-
-    def clear_own(i):
-        r.ml_own[i] = empty
-
-    loop(0, count, clear_own)
-    loop(0, count, combine)
 
     def ml_copy(s):
         return remote(
@@ -514,14 +589,6 @@
             r.sem_ml_r.at[s],
             head * share + (turn + s) % share,
         )
-
-    for s in range(1, share):
-        ml_copy(s).start()
-    arrive(2)
-    g_chunk(2)
-    for s in range(1, share):
-        ml_copy(s).wait_recv()
-        ml_copy(s).wait_send()
 
     def join(i):
         peaks = [r.ml_own[i, 0:1, :]] + [r.ml_got[s, i, 0:1, :] for s in range(share - 1)]
@@ -533,8 +600,6 @@
         r.ml_own[i, 0:1, :] = peak
         r.ml_own[i, 1:2, :] = 1.0 / total
 
-    loop(0, count, join)
-
     def normal(n):
         mine = p.own(n, turn)
         first = p.offset(n, turn)
@@ -546,11 +611,6 @@
             r.cache[first + i - mine] = (e * weight).astype(BF16)
 
         loop(mine, count, one)
-
-    loop(0, heads, normal)
-    settle(2)
-
-    loop(1, far, lambda d: far_copy(d).wait_recv())
 
     def far_sum(g):
         rate = column(r.rate, g)
@@ -566,200 +626,6 @@
             behind = behind + decay(rate, gap, source > my_far) * got
         r.st_fin[0, lines, :] += ahead
         r.st_fin[1, lines, :] += behind
-
-    loop(0, p.groups, far_sum)
-
-    gf = (r.sem_gf_s, r.sem_gf_r)
-
-    def g_hand(n, s, arriving):
-        source = (turn - s + share) % share if arriving else turn
-        part = pl.ds(source * heads * 2, heads * 2)
-        return remote(
-            r.g_all.at[part],
-            r.g_all.at[part],
-            gf[0].at[n, s],
-            gf[1].at[n, s],
-            head * share + (turn + s) % share,
-        )
-
-    for n in range(3, p.chunks):
-        g_chunk(n)
-    fetch_o.wait()
-    ones = jnp.ones((8, HD), BF16)
-
-    def delta_of(h):
-        prod = r.g_low[:, cols(h)].astype(F32) * r.o_buf[:, cols(h)].astype(F32)
-        high, low = split(prod)
-        value = dot_nt(ones, high) + dot_nt(ones, low)
-        r.delta_out[h, 0] = value[:, :half]
-        r.delta_out[h, 1] = value[:, half:]
-
-    loop(0, heads, delta_of)
-
-    def delta_copy(d, arriving):
-        to = (head + d) % heads
-        source = (head - d + heads) % heads if arriving else head
-        return remote(
-            r.delta_out.at[to],
-            r.delta_all.at[pl.ds((turn * heads + source) * 2, 2)],
-            r.sem_d_s.at[d],
-            r.sem_d_r.at[d],
-            to * share + turn,
-        )
-
-    loop(1, heads, lambda d: delta_copy(d, False).start())
-    r.delta_all[pl.ds((turn * heads + head) * 2, 2)] = r.delta_out[head]
-
-    def delta_hand(s, arriving):
-        source = (turn - s + share) % share if arriving else turn
-        part = pl.ds(source * heads * 2, heads * 2)
-        return remote(
-            r.delta_all.at[part],
-            r.delta_all.at[part],
-            r.sem_df_s.at[s],
-            r.sem_df_r.at[s],
-            head * share + (turn + s) % share,
-        )
-
-    for n in range(p.chunks):
-        g_arrive(n)
-    for s in range(1, share):
-        g_hand(0, s, False).start()
-    loop(1, heads, lambda d: delta_copy(d, True).wait_recv())
-    for s in range(1, share):
-        delta_hand(s, False).start()
-    for s in range(1, share):
-        g_hand(0, s, True).wait_recv()
-        delta_hand(s, True).wait_recv()
-    in_order(r.g_all, r.g_seq)
-
-    def order_delta(place):
-        r.delta_seq[place] = r.delta_all[r.table[0, place]]
-
-    loop(0, 2 * count, order_delta)
-
-    def column_pass(kind, other, target, factor):
-        def one(n):
-            mine = p.own(n, turn)
-            first = p.offset(n, turn)
-
-            def add(i, acc):
-                return acc + dot_nn(r.cache[first + i - mine], other[rows_at(i, tok), :])
-
-            acc = lax.fori_loop(mine, count, add, jnp.zeros((tok, HD), F32))
-            value = (acc * factor).astype(BF16)
-            target[2 * mine] = value[:half]
-            target[2 * mine + 1] = value[half:]
-            for s in range(1, share):
-                kv_copy(kind, n, s, target, False).start()
-
-        loop(0, heads, one)
-
-    def kv_copy(kind, n, s, target, arriving):
-        source = (turn - s + share) % share if arriving else turn
-        rows = pair_at(p.own(n, source))
-        return remote(
-            target.at[rows],
-            target.at[rows],
-            r.sem_kv_s.at[kind, n, s],
-            r.sem_kv_r.at[kind, n, s],
-            head * share + (turn + s) % share,
-        )
-
-    def kv_arrive(kind, target):
-        def one(n):
-            for s in range(1, share):
-                kv_copy(kind, n, s, target, True).wait_recv()
-
-        loop(0, heads, one)
-
-    outs = (r.out_q, r.out_k, r.out_v)
-
-    def res_copy(kind, d):
-        to = (head + d) % heads
-        return remote(
-            r.send.at[kind, d],
-            outs[kind].at[:, :, cols(head)],
-            r.sem_res_s.at[kind, d],
-            r.sem_res_r.at[kind, d],
-            to * share + turn,
-        )
-
-    def res_local(kind):
-        return local(r.send.at[kind, 0], outs[kind].at[:, :, cols(head)], r.sem_out.at[kind])
-
-    def hand_back(kind, value_of):
-        def one(d):
-            flat = (turn * heads + (head + d) % heads) * 2
-            for b in range(2):
-                place = r.table[1, flat + b]
-                value = value_of(place, (head + d) % heads, b)
-                r.send[kind, d, b] = value
-
-        def both(d):
-            one(d)
-            res_copy(kind, d).start()
-
-        loop(1, heads, both)
-        one(0)
-        res_local(kind).start()
-
-    column_pass(0, r.g_seq, r.dv_seq, 1.0)
-    kv_arrive(0, r.dv_seq)
-    hand_back(2, lambda place, h, b: r.dv_seq[place])
-
-    def row_pass(i):
-        g = r.g_seq[rows_at(i, tok), :]
-        delta = jnp.concatenate(
-            [r.delta_seq[2 * i, 0:1, :], r.delta_seq[2 * i + 1, 0:1, :]], axis=1
-        )
-
-        def one(n, acc):
-            mine = p.own(n, turn)
-            where = p.offset(n, turn) + i - mine
-            grad_prob = dot_nt(r.v_seq[rows_at(mine, tok), :], g)
-            grad_score = (r.cache[where].astype(F32) * (grad_prob - delta)).astype(BF16)
-            r.cache[where] = grad_score
-            return acc + dot_nn(r.k_turn[n], grad_score)
-
-        acc = lax.fori_loop(0, p.held(i, turn), one, jnp.zeros((HD, tok), F32))
-        value = acc.T * SCALE
-        r.dq_seq[2 * i] = value[:half]
-        r.dq_seq[2 * i + 1] = value[half:]
-
-    loop(0, count, row_pass)
-
-    def q_copy(s):
-        return remote(
-            r.dq_out.at[s - 1],
-            r.dq_got.at[s - 1],
-            r.sem_q_s.at[s],
-            r.sem_q_r.at[s],
-            head * share + (turn + s) % share,
-        )
-
-    for s in range(1, share):
-
-        def pick(f, s=s):
-            place = r.table[1, (turn + s) % share * heads * 2 + f]
-            r.dq_out[s - 1, f] = r.dq_seq[place]
-
-        loop(0, 2 * heads, pick)
-        q_copy(s).start()
-
-    column_pass(1, r.q_seq, r.dk_seq, SCALE)
-    for s in range(1, share):
-        q_copy(s).wait_recv()
-
-    def dq_value(place, h, b):
-        value = r.dq_seq[place]
-        for s in range(1, share):
-            value = value + r.dq_got[s - 1, 2 * h + b]
-        return value.astype(BF16)
-
-    hand_back(0, dq_value)
-    kv_arrive(1, r.dk_seq)
-    hand_back(1, lambda place, h, b: r.dk_seq[place])
 
     lag_id = lax.broadcasted_iota(jnp.int32, lane_shape, 1)
     turned = jnp.where(lag_id == 0, 0, tok - lag_id).astype(F32)
@@ -812,11 +678,188 @@
         r.hy_out[1, :, here] = (mid * v).astype(BF16)
         r.hy_out[2, :, here] = (mid * k).astype(BF16)
 
-    loop(0, p.groups, mix)
     hy_outs = (r.out_hq, r.out_hk, r.out_hv)
     give = [local(r.hy_out.at[i], hy_outs[i], r.sem_out.at[3 + i]) for i in range(3)]
+
+    for c in fetch_rest:
+        c.wait()
+    g_chunk(0)
+    arrive(0)
+    arrive(1)
+    loop(1, heads, lambda d: in_copy(2, d, False).start())
+    settle(0)
+    settle(1)
+    g_arrive(0)
+    loop(0, heads, turn_keys)
+    loop(0, heads, spread)
+    loop(0, count, combine)
+    for s in range(1, share):
+        ml_copy(s).start()
+    g_chunk(1)
+    fetch_o.wait()
+    delta_half(0)
+    for s in range(1, share):
+        ml_copy(s).wait_recv()
+        ml_copy(s).wait_send()
+    loop(0, count, join)
+    loop(0, heads, normal)
+    g_arrive(1)
+    delta_arrive(0)
+    loop(1, far, lambda d: far_copy(d).wait_recv())
+    loop(0, p.groups, far_sum)
+    g_chunk(2)
+    loop(0, p.groups, mix)
     for c in give:
         c.start()
+    arrive(2)
+    g_arrive(2)
+    settle(2)
+    g_chunk(3)
+    delta_half(1)
+    g_arrive(3)
+    delta_arrive(1)
+    for s in range(1, share):
+        for n in range(p.chunks):
+            g_hand(n, s, True).wait_recv()
+        for b in range(2):
+            delta_hand(b, s, True).wait_recv()
+    in_order(r.g_all, r.g_seq, 1)
+
+    def order_delta(i):
+        for b in range(2):
+            r.delta_row[i, :, b * half : (b + 1) * half] = r.delta_all[r.table[1, 2 * i + b]]
+
+    loop(0, count, order_delta)
+
+    def keep(kind, n, target, value):
+        mine = p.own(n, turn)
+        target[2 * mine] = value[:half]
+        target[2 * mine + 1] = value[half:]
+        for s in range(1, share):
+            kv_copy(kind, n, s, target, False).start()
+
+    def value_pass(n):
+        mine = p.own(n, turn)
+        first = p.offset(n, turn) - mine
+
+        def some(i, width, acc):
+            probs = jnp.concatenate([r.cache[first + i + u] for u in range(width)], axis=1)
+            return acc + dot_nn(probs, r.g_seq[pl.ds(pl.multiple_of(i * tok, tok), width * tok), :])
+
+        acc = spans(mine, count, some, jnp.zeros((tok, HD), F32))
+        keep(0, n, r.dv_seq, acc.astype(BF16))
+
+    def kv_copy(kind, n, s, target, arriving):
+        source = (turn - s + share) % share if arriving else turn
+        rows = pair_at(p.own(n, source))
+        return remote(
+            target.at[rows],
+            target.at[rows],
+            r.sem_kv_s.at[kind, n, s],
+            r.sem_kv_r.at[kind, n, s],
+            head * share + (turn + s) % share,
+        )
+
+    def kv_arrive(kind, target):
+        def one(n):
+            for s in range(1, share):
+                kv_copy(kind, n, s, target, True).wait_recv()
+
+        loop(0, heads, one)
+
+    outs = (r.out_q, r.out_k, r.out_v)
+
+    def res_copy(kind, d):
+        to = (head + d) % heads
+        return remote(
+            r.send.at[kind, d],
+            outs[kind].at[:, :, cols(head)],
+            r.sem_res_s.at[kind, d],
+            r.sem_res_r.at[kind, d],
+            to * share + turn,
+        )
+
+    def res_local(kind):
+        return local(r.send.at[kind, 0], outs[kind].at[:, :, cols(head)], r.sem_out.at[kind])
+
+    def hand_back(kind, value_of):
+        def one(d):
+            flat = (turn * heads + (head + d) % heads) * 2
+            for b in range(2):
+                place = place_of(flat + b)
+                value = value_of(place, (head + d) % heads, b)
+                r.send[kind, d, b] = value
+
+        def both(d):
+            one(d)
+            res_copy(kind, d).start()
+
+        loop(1, heads, both)
+        one(0)
+        res_local(kind).start()
+
+    loop(0, heads, value_pass)
+    kv_arrive(0, r.dv_seq)
+    hand_back(2, lambda place, h, b: r.dv_seq[place])
+
+    def score_pass(n):
+        mine = p.own(n, turn)
+        first = p.offset(n, turn) - mine
+        keys = rows_at(mine, tok)
+
+        def some(i, width, acc):
+            scores = []
+            for u in range(width):
+                grad_prob = dot_nt(r.v_seq[keys, :], r.g_seq[rows_at(i + u, tok), :])
+                change = grad_prob - r.delta_row[i + u, 0:1, :]
+                score = (r.cache[first + i + u].astype(F32) * change).astype(BF16)
+                r.dq_turn[i + u] += dot_nn(r.k_turn[n], score)
+                scores.append(score)
+            queries = r.q_seq[pl.ds(pl.multiple_of(i * tok, tok), width * tok), :]
+            return acc + dot_nn(jnp.concatenate(scores, axis=1), queries)
+
+        acc = spans(mine, count, some, jnp.zeros((tok, HD), F32))
+        keep(1, n, r.dk_seq, (acc * SCALE).astype(BF16))
+
+    loop(0, heads, score_pass)
+
+    def turn_queries(i):
+        value = r.dq_turn[i].T * SCALE
+        r.dq_seq[2 * i] = value[:half]
+        r.dq_seq[2 * i + 1] = value[half:]
+
+    loop(0, count, turn_queries)
+
+    def q_copy(s):
+        return remote(
+            r.dq_out.at[s - 1],
+            r.dq_got.at[s - 1],
+            r.sem_q_s.at[s],
+            r.sem_q_r.at[s],
+            head * share + (turn + s) % share,
+        )
+
+    for s in range(1, share):
+
+        def pick(f, s=s):
+            place = place_of((turn + s) % share * heads * 2 + f)
+            r.dq_out[s - 1, f] = r.dq_seq[place]
+
+        loop(0, 2 * heads, pick)
+        q_copy(s).start()
+
+    kv_arrive(1, r.dk_seq)
+    hand_back(1, lambda place, h, b: r.dk_seq[place])
+    for s in range(1, share):
+        q_copy(s).wait_recv()
+
+    def dq_value(place, h, b):
+        value = r.dq_seq[place]
+        for s in range(1, share):
+            value = value + r.dq_got[s - 1, 2 * h + b]
+        return value.astype(BF16)
+
+    hand_back(0, dq_value)
 
     for n in range(p.chunks):
         for d in range(1, p.parts):
@@ -829,10 +872,13 @@
             hand_on(alls[i], i, s, False, fw).wait_send()
     for n in range(p.chunks):
         loop(1, heads, lambda d, n=n: g_copy(n, d, False).wait_send())
-    loop(1, heads, lambda d: delta_copy(d, False).wait_send())
+    for b in range(2):
+        loop(1, heads, lambda d, b=b: delta_copy(b, d, False).wait_send())
     for s in range(1, share):
-        g_hand(0, s, False).wait_send()
-        delta_hand(s, False).wait_send()
+        for n in range(p.chunks):
+            g_hand(n, s, False).wait_send()
+        for b in range(2):
+            delta_hand(b, s, False).wait_send()
         q_copy(s).wait_send()
 
         def kv_sent(n, s=s):
@@ -846,6 +892,28 @@
         res_local(kind).wait()
     for c in give:
         c.wait()
+
+
+def copy_kernel(*refs):
+    sources, targets, held, (sem_in, sem_out) = refs[:6], refs[6:12], refs[12:18], refs[18:]
+    into, out = [], []
+    for i in range(6):
+        size = held[i].shape[0] // 2
+        for j in range(2):
+            part = pl.ds(j * size, size)
+            into.append(
+                pltpu.make_async_copy(sources[i].at[part], held[i].at[part], sem_in.at[i, j])
+            )
+            out.append(
+                pltpu.make_async_copy(held[i].at[part], targets[i].at[part], sem_out.at[i, j])
+            )
+    for c in into:
+        c.start()
+    for c, d in zip(into, out, strict=True):
+        c.wait()
+        d.start()
+    for d in out:
+        d.wait()
 
 
 def body(
@@ -868,10 +936,6 @@
     modes, groups = filter_rate.shape
     count, parts = lax.axis_size("ctx"), lax.axis_size("tp")
     p = Plan(count, parts, tok, feat, attn_dy.shape[1], chan, modes, groups)
-    places = block_place.reshape(p.heads, p.share, 2).transpose(1, 0, 2).reshape(-1)
-    slot = jnp.arange(2 * count, dtype=jnp.int32)
-    found = jnp.where(places[None, :] == slot[:, None], slot[None, :], 0)
-    table = jnp.stack([jnp.sum(found, axis=1), places])
     items = scratch(p)
     names = INPUTS + OUTPUTS + tuple(items)
     hbm = pl.BlockSpec(memory_space=pl.ANY)
@@ -889,7 +953,7 @@
         ),
         name="grads",
     )(
-        table,
+        block_place,
         filter_rate,
         filter_residue,
         attn_q.reshape(2, p.half, feat),
@@ -903,6 +967,16 @@
         hyena_v,
         hyena_dy,
     )
+    outs = pl.pallas_call(
+        copy_kernel,
+        in_specs=[hbm] * 6,
+        out_specs=[hbm] * 6,
+        out_shape=[attn_out] * 3 + [hy_out] * 3,
+        scratch_shapes=[pltpu.VMEM(attn_out.shape, BF16)] * 3
+        + [pltpu.VMEM(hy_out.shape, BF16)] * 3
+        + [pltpu.SemaphoreType.DMA((6, 2))] * 2,
+        name="results",
+    )(*outs)
     return tuple(x.reshape(tok, feat) for x in outs[:3]) + tuple(outs[3:])
 
 

time: 180 us -> 153 us (0.85)
  local copies, waits for them, and re-layouts: 13.4 us -> 0 us
  Pallas kernels: 165 us -> 152 us
    pallas_call x1, Pallas kernels: 165 us -> 147 us  [body(): pl.pallas_call(functools.partial(kernel, p, names), in_specs=[pl.BlockSpe...]
    unnamed x6 -> x0, local copies, waits for them, and re-layouts: 12.5 us -> none
    pallas_call x0 -> x1, Pallas kernels: none -> 4.43 us  [body(): pl.pallas_call(copy_kernel, in_specs=[hbm] * 6, out_specs=[hbm] * 6, out_...]
where the time goes in v1:
time: 153 us; the launch traced here: 152 us
  Pallas kernels  152 us (99%)
    pallas_call x1, Pallas kernels, body(): pl.pallas_call(functools.partial(kernel, p, names), in_specs=[pl.BlockSpe...  147 us
    pallas_call x1, Pallas kernels, body(): pl.pallas_call(copy_kernel, in_specs=[hbm] * 6, out_specs=[hbm] * 6, out_...  4.43 us

profile of v1, /device:TPU:13, one launch (start us, length us, event | category | flops | bytes accessed | tf_op | source)
XLA Modules:
  0.0 152.5 jit_solution(824141537113997030)
XLA Ops:
  0.6 147.4 %grads.1 = (bf16[2,128,1024]{2,1,0:T(8,128)(2,1)}, bf16[2,128,1024]{2,1,0:T(8,128)(2,1)}, bf16[2,128,1024]{2,1,0:T(8,128)(2,1)}, bf16[256,2048]{1,0:T(8,128)(2,1...) custom-call(s32[32]{0:T(128)} %refs_0_.1, f32[16,16]{1,0:T(8,128)} %refs_1_.1, f32[16,16]{1,0:T(8,128)} %refs_2_.1, ...), custom_call_target="tpu_custom_call" | custom-call | tf_op jit(solution)/shard_map/grads/pallas_call | solution.py:945
  148.0 4.4 %results.1 = (bf16[2,128,1024]{2,1,0:T(8,128)(2,1)}, bf16[2,128,1024]{2,1,0:T(8,128)(2,1)}, bf16[2,128,1024]{2,1,0:T(8,128)(2,1)}, bf16[256,2048]{1,0:T(8,128)(2...) custom-call(bf16[2,128,1024]{2,1,0:T(8,128)(2,1)} %get-tuple-element.18.refs_0_, ...), custom_call_target="tpu_custom_call" | custom-call | tf_op jit(solution)/shard_map/results/pallas_call | solution.py:970

commit v2 on v1

--- a/solution.py
+++ b/solution.py
@@ -124,10 +124,9 @@
         ml=vm((p.heads * p.count, 8, p.tok), F32),
         ml_own=vm((p.count, 8, p.tok), F32),
         ml_got=vm((other, p.count, 8, p.tok), F32),
-        dq_turn=vm((p.count, HD, p.tok), F32),
         dq_seq=vm((2 * p.count, p.half, HD), F32),
-        dq_out=vm((other, 2 * p.heads, p.half, HD), F32),
-        dq_got=vm((other, 2 * p.heads, p.half, HD), F32),
+        dq_out=vm((other, 2 * p.heads, p.half, HD), BF16),
+        dq_got=vm((other, 2 * p.heads, p.half, HD), BF16),
         dk_seq=blocked,
         dv_seq=blocked,
         send=vm((3, p.heads, 2, p.half, HD), BF16),
@@ -145,8 +144,8 @@
         sem_dy_r=dma((rest, p.chunks)),
         sem_in_s=dma((3, p.heads)),
         sem_in_r=dma((3, p.heads)),
-        sem_fw_s=dma((3, p.share)),
-        sem_fw_r=dma((3, p.share)),
+        sem_fw_s=dma((3, p.heads, p.share)),
+        sem_fw_r=dma((3, p.heads, p.share)),
         sem_g_s=dma((p.chunks, p.heads)),
         sem_g_r=dma((p.chunks, p.heads)),
         sem_gf_s=dma((p.chunks, p.share)),
@@ -348,8 +347,234 @@
 
     loop(0, p.feat // p.tile, own_product)
 
-    loop(1, near, lambda d: near_copy(d, True).wait_recv())
-    r.st_got[my_near] = r.st_own[...]
+    def place_of(flat):
+        source, h = flat // (2 * heads), flat // 2 % heads
+        return r.places[(h * share + source) * 2 + flat % 2]
+
+    def find(place):
+        slot = jnp.int32(0)
+        for stored in range(2 * count):
+            c, b = divmod(stored, 2)
+            flat = c % share * heads + c // share
+            slot = jnp.where(r.places[stored] == place, 2 * flat + b, slot)
+        r.table[0, place] = slot
+        r.table[1, place] = slot % 2 * count + slot // 2
+
+    loop(0, 2 * count, find)
+
+    row_id = lax.broadcasted_iota(jnp.int32, (8, tok), 0)
+    empty = jnp.where(row_id == 0, NEG_LARGE, 0.0)
+
+    def clear(n):
+        r.ml[n] = empty
+
+    loop(0, heads * count, clear)
+
+    def hand_on(i, d, s, arriving):
+        source = (turn - s + share) % share if arriving else turn
+        slot = pair_at(source * heads + (head - d + heads) % heads)
+        return remote(
+            alls[i].at[slot],
+            alls[i].at[slot],
+            r.sem_fw_s.at[i, d, s],
+            r.sem_fw_r.at[i, d, s],
+            head * share + (turn + s) % share,
+        )
+
+    def arrive(*kinds):
+        for i in kinds:
+            fetch_own[i].wait()
+            for s in range(1, share):
+                hand_on(i, 0, s, False).start()
+
+        def one(d):
+            for i in kinds:
+                in_copy(i, d, True).wait_recv()
+                for s in range(1, share):
+                    hand_on(i, d, s, False).start()
+
+        loop(1, heads, one)
+
+    def in_order(source, target, row):
+        def one(place):
+            target[rows_at(place, half), :] = source[r.table[row, place]]
+
+        loop(0, 2 * count, one)
+
+    def settle(i):
+        for s in range(1, share):
+            loop(0, heads, lambda d, s=s: hand_on(i, d, s, True).wait_recv())
+        in_order(alls[i], seqs[i], 0)
+
+    def g_place(n, source):
+        slot, start = divmod(n * p.piece, half)
+        return slot * count + turn * heads + source, pl.ds(start, p.piece)
+
+    def g_copy(n, d, arriving):
+        to = (head + d) % heads
+        source = (head - d + heads) % heads if arriving else head
+        rows = pl.ds(n * p.piece, p.piece)
+        slot, inner = g_place(n, source)
+        return remote(
+            r.g_low.at[rows, cols(to)],
+            r.g_all.at[slot, inner, :],
+            r.sem_g_s.at[n, d],
+            r.sem_g_r.at[n, d],
+            to * share + turn,
+        )
+
+    def g_chunks(start, stop):
+        for n in range(start, stop):
+            for d in range(1, p.parts):
+                dy_copy(d, n).wait_recv()
+        rows = pl.ds(start * p.piece, (stop - start) * p.piece)
+
+        def tile(c):
+            at_cols = rows_at(c, p.tile)
+            total = r.g_part[rows, at_cols]
+            for d in range(1, p.parts):
+                total = total + dot_nt(r.dy_got[d - 1, rows, :], r.w_rest[d - 1, at_cols, :])
+            r.g_low[rows, at_cols] = total.astype(BF16)
+
+        loop(0, p.feat // p.tile, tile)
+        for n in range(start, stop):
+            loop(1, heads, lambda d, n=n: g_copy(n, d, False).start())
+        for n in range(start, stop):
+            slot, inner = g_place(n, head)
+            r.g_all[slot, inner, :] = r.g_low[pl.ds(n * p.piece, p.piece), cols(head)]
+
+    def g_hand(n, s, arriving):
+        source = (turn - s + share) % share if arriving else turn
+        slot, start = divmod(n * p.piece, half)
+        part = r.g_all.at[
+            pl.ds(slot * count + source * heads, heads), pl.ds(start, p.piece), :
+        ]
+        return remote(
+            part,
+            part,
+            r.sem_gf_s.at[n, s],
+            r.sem_gf_r.at[n, s],
+            head * share + (turn + s) % share,
+        )
+
+    def g_arrive(n):
+        loop(1, heads, lambda d: g_copy(n, d, True).wait_recv())
+        for s in range(1, share):
+            g_hand(n, s, False).start()
+
+    ones = jnp.ones((8, HD), BF16)
+
+    def delta_copy(b, d, arriving):
+        to = (head + d) % heads
+        source = (head - d + heads) % heads if arriving else head
+        return remote(
+            r.delta_out.at[b, to],
+            r.delta_all.at[b * count + turn * heads + source],
+            r.sem_d_s.at[b, d],
+            r.sem_d_r.at[b, d],
+            to * share + turn,
+        )
+
+    def delta_half(b):
+        rows = pl.ds(b * half, half)
+
+        def one(h):
+            prod = r.g_low[rows, cols(h)].astype(F32) * r.o_buf[rows, cols(h)].astype(F32)
+            high, low = split(prod)
+            r.delta_out[b, h] = dot_nt(ones, high) + dot_nt(ones, low)
+
+        loop(0, heads, one)
+        loop(1, heads, lambda d: delta_copy(b, d, False).start())
+        r.delta_all[b * count + turn * heads + head] = r.delta_out[b, head]
+
+    def delta_hand(b, s, arriving):
+        source = (turn - s + share) % share if arriving else turn
+        part = r.delta_all.at[pl.ds(b * count + source * heads, heads)]
+        return remote(
+            part,
+            part,
+            r.sem_df_s.at[b, s],
+            r.sem_df_r.at[b, s],
+            head * share + (turn + s) % share,
+        )
+
+    def delta_arrive(b):
+        loop(1, heads, lambda d: delta_copy(b, d, True).wait_recv())
+        for s in range(1, share):
+            delta_hand(b, s, False).start()
+
+    square = (tok, tok)
+
+    def turn_keys(n):
+        mine = p.own(n, turn)
+        r.k_turn[n] = r.k_seq[rows_at(mine, tok), :].astype(F32).T.astype(BF16)
+
+    def spread(n):
+        mine = p.own(n, turn)
+        first = p.offset(n, turn)
+        keys = rows_at(mine, tok)
+
+        def one(i, masked=False):
+            s = dot_nt(r.k_seq[keys, :], r.q_seq[rows_at(i, tok), :])
+            if masked:
+                key_id = lax.broadcasted_iota(jnp.int32, square, 0)
+                query_id = lax.broadcasted_iota(jnp.int32, square, 1)
+                s = jnp.where(key_id <= query_id, s, NEG_LARGE)
+            peak = jnp.max(s, axis=0, keepdims=True)
+            e = jnp.exp2((s - peak) * LN2_SCALE)
+            r.cache[first + i - mine] = e.astype(BF16)
+            r.ml[n * count + i, 0:1, :] = peak
+            r.ml[n * count + i, 1:2, :] = jnp.sum(e, axis=0, keepdims=True)
+
+        def some(i, width, carry):
+            for u in range(width):
+                one(i + u)
+            return carry
+
+        one(mine, True)
+        spans(mine + 1, count, some)
+
+    def combine(i):
+        peaks = [r.ml[n * count + i, 0:1, :] for n in range(heads)]
+        peak = functools.reduce(jnp.maximum, peaks)
+        total = 0.0
+        for n in range(heads):
+            weight = jnp.exp2((peaks[n] - peak) * LN2_SCALE)
+            total = total + weight * r.ml[n * count + i, 1:2, :]
+        r.ml_own[i] = empty
+        r.ml_own[i, 0:1, :] = peak
+        r.ml_own[i, 1:2, :] = total
+
+    def ml_copy(s):
+        return remote(
+            r.ml_own,
+            r.ml_got.at[s - 1],
+            r.sem_ml_s.at[s],
+            r.sem_ml_r.at[s],
+            head * share + (turn + s) % share,
+        )
+
+    def join(i):
+        peaks = [r.ml_own[i, 0:1, :]] + [r.ml_got[s, i, 0:1, :] for s in range(share - 1)]
+        peak = functools.reduce(jnp.maximum, peaks)
+        total = jnp.exp2((peaks[0] - peak) * LN2_SCALE) * r.ml_own[i, 1:2, :]
+        for s in range(share - 1):
+            weight = jnp.exp2((peaks[s + 1] - peak) * LN2_SCALE)
+            total = total + weight * r.ml_got[s, i, 1:2, :]
+        r.ml_own[i, 0:1, :] = peak
+        r.ml_own[i, 1:2, :] = 1.0 / total
+
+    def normal(n):
+        mine = p.own(n, turn)
+        first = p.offset(n, turn)
+
+        def one(i):
+            weight = jnp.exp2((r.ml[n * count + i, 0:1, :] - r.ml_own[i, 0:1, :]) * LN2_SCALE)
+            weight = weight * r.ml_own[i, 1:2, :]
+            e = r.cache[first + i - mine].astype(F32)
+            r.cache[first + i - mine] = (e * weight).astype(BF16)
+
+        loop(mine, count, one)
 
     def decay(rate, steps, good):
         power = jnp.exp(-rate * (tok * jnp.maximum(steps, 0)).astype(F32))
@@ -374,8 +599,6 @@
         r.st_fin[0, lines, :] = fin
         r.st_fin[1, lines, :] = fin_back
 
-    loop(0, p.groups, near_sum)
-
     def far_copy(d):
         to = (my_far + d) % far
         return remote(
@@ -385,232 +608,6 @@
             r.sem_far_r.at[d],
             to * near + my_near,
         )
-
-    loop(1, far, lambda d: far_copy(d).start())
-
-    def place_of(flat):
-        source, h = flat // (2 * heads), flat // 2 % heads
-        return r.places[(h * share + source) * 2 + flat % 2]
-
-    def find(place):
-        slot = jnp.int32(0)
-        for stored in range(2 * count):
-            c, b = divmod(stored, 2)
-            flat = c % share * heads + c // share
-            slot = jnp.where(r.places[stored] == place, 2 * flat + b, slot)
-        r.table[0, place] = slot
-        r.table[1, place] = slot % 2 * count + slot // 2
-
-    loop(0, 2 * count, find)
-
-    def clear_queries(i):
-        r.dq_turn[i] = jnp.zeros((HD, tok), F32)
-
-    loop(0, count, clear_queries)
-    row_id = lax.broadcasted_iota(jnp.int32, (8, tok), 0)
-    empty = jnp.where(row_id == 0, NEG_LARGE, 0.0)
-
-    def clear(n):
-        r.ml[n] = empty
-
-    loop(0, heads * count, clear)
-
-    def hand_on(ref, i, s, arriving, sems):
-        source = (turn - s + share) % share if arriving else turn
-        part = pl.ds(source * heads * 2, heads * 2)
-        return remote(
-            ref.at[part],
-            ref.at[part],
-            sems[0].at[i, s],
-            sems[1].at[i, s],
-            head * share + (turn + s) % share,
-        )
-
-    fw = (r.sem_fw_s, r.sem_fw_r)
-
-    def arrive(i):
-        loop(1, heads, lambda d: in_copy(i, d, True).wait_recv())
-        fetch_own[i].wait()
-        for s in range(1, share):
-            hand_on(alls[i], i, s, False, fw).start()
-
-    def in_order(source, target, row):
-        def one(place):
-            target[rows_at(place, half), :] = source[r.table[row, place]]
-
-        loop(0, 2 * count, one)
-
-    def settle(i):
-        for s in range(1, share):
-            hand_on(alls[i], i, s, True, fw).wait_recv()
-        in_order(alls[i], seqs[i], 0)
-
-    def g_place(n, source):
-        slot, start = divmod(n * p.piece, half)
-        return slot * count + turn * heads + source, pl.ds(start, p.piece)
-
-    def g_copy(n, d, arriving):
-        to = (head + d) % heads
-        source = (head - d + heads) % heads if arriving else head
-        rows = pl.ds(n * p.piece, p.piece)
-        slot, inner = g_place(n, source)
-        return remote(
-            r.g_low.at[rows, cols(to)],
-            r.g_all.at[slot, inner, :],
-            r.sem_g_s.at[n, d],
-            r.sem_g_r.at[n, d],
-            to * share + turn,
-        )
-
-    def g_chunk(n):
-        for d in range(1, p.parts):
-            dy_copy(d, n).wait_recv()
-        rows = pl.ds(n * p.piece, p.piece)
-
-        def tile(c):
-            at_cols = rows_at(c, p.tile)
-            total = dot_nt(r.w_rest[0, at_cols, :], r.dy_got[0, rows, :])
-            for d in range(2, p.parts):
-                total = total + dot_nt(r.w_rest[d - 1, at_cols, :], r.dy_got[d - 1, rows, :])
-            r.g_low[rows, at_cols] = (r.g_part[rows, at_cols] + total.T).astype(BF16)
-
-        loop(0, p.feat // p.tile, tile)
-        loop(1, heads, lambda d: g_copy(n, d, False).start())
-        slot, inner = g_place(n, head)
-        r.g_all[slot, inner, :] = r.g_low[rows, cols(head)]
-
-    def g_hand(n, s, arriving):
-        source = (turn - s + share) % share if arriving else turn
-        slot, start = divmod(n * p.piece, half)
-        part = r.g_all.at[
-            pl.ds(slot * count + source * heads, heads), pl.ds(start, p.piece), :
-        ]
-        return remote(
-            part,
-            part,
-            r.sem_gf_s.at[n, s],
-            r.sem_gf_r.at[n, s],
-            head * share + (turn + s) % share,
-        )
-
-    def g_arrive(n):
-        loop(1, heads, lambda d: g_copy(n, d, True).wait_recv())
-        for s in range(1, share):
-            g_hand(n, s, False).start()
-
-    ones = jnp.ones((8, HD), BF16)
-
-    def delta_copy(b, d, arriving):
-        to = (head + d) % heads
-        source = (head - d + heads) % heads if arriving else head
-        return remote(
-            r.delta_out.at[b, to],
-            r.delta_all.at[b * count + turn * heads + source],
-            r.sem_d_s.at[b, d],
-            r.sem_d_r.at[b, d],
-            to * share + turn,
-        )
-
-    def delta_half(b):
-        rows = pl.ds(b * half, half)
-
-        def one(h):
-            prod = r.g_low[rows, cols(h)].astype(F32) * r.o_buf[rows, cols(h)].astype(F32)
-            high, low = split(prod)
-            r.delta_out[b, h] = dot_nt(ones, high) + dot_nt(ones, low)
-
-        loop(0, heads, one)
-        loop(1, heads, lambda d: delta_copy(b, d, False).start())
-        r.delta_all[b * count + turn * heads + head] = r.delta_out[b, head]
-
-    def delta_hand(b, s, arriving):
-        source = (turn - s + share) % share if arriving else turn
-        part = r.delta_all.at[pl.ds(b * count + source * heads, heads)]
-        return remote(
-            part,
-            part,
-            r.sem_df_s.at[b, s],
-            r.sem_df_r.at[b, s],
-            head * share + (turn + s) % share,
-        )
-
-    def delta_arrive(b):
-        loop(1, heads, lambda d: delta_copy(b, d, True).wait_recv())
-        for s in range(1, share):
-            delta_hand(b, s, False).start()
-
-    square = (tok, tok)
-
-    def turn_keys(n):
-        mine = p.own(n, turn)
-        r.k_turn[n] = r.k_seq[rows_at(mine, tok), :].astype(F32).T.astype(BF16)
-
-    def spread(n):
-        mine = p.own(n, turn)
-        first = p.offset(n, turn)
-        keys = rows_at(mine, tok)
-
-        def one(i, masked=False):
-            s = dot_nt(r.k_seq[keys, :], r.q_seq[rows_at(i, tok), :])
-            if masked:
-                key_id = lax.broadcasted_iota(jnp.int32, square, 0)
-                query_id = lax.broadcasted_iota(jnp.int32, square, 1)
-                s = jnp.where(key_id <= query_id, s, NEG_LARGE)
-            peak = jnp.max(s, axis=0, keepdims=True)
-            e = jnp.exp2((s - peak) * LN2_SCALE)
-            r.cache[first + i - mine] = e.astype(BF16)
-            r.ml[n * count + i, 0:1, :] = peak
-            r.ml[n * count + i, 1:2, :] = jnp.sum(e, axis=0, keepdims=True)
-
-        def some(i, width, carry):
-            for u in range(width):
-                one(i + u)
-            return carry
-
-        one(mine, True)
-        spans(mine + 1, count, some)
-
-    def combine(i):
-        peaks = [r.ml[n * count + i, 0:1, :] for n in range(heads)]
-        peak = functools.reduce(jnp.maximum, peaks)
-        total = 0.0
-        for n in range(heads):
-            weight = jnp.exp2((peaks[n] - peak) * LN2_SCALE)
-            total = total + weight * r.ml[n * count + i, 1:2, :]
-        r.ml_own[i] = empty
-        r.ml_own[i, 0:1, :] = peak
-        r.ml_own[i, 1:2, :] = total
-
-    def ml_copy(s):
-        return remote(
-            r.ml_own,
-            r.ml_got.at[s - 1],
-            r.sem_ml_s.at[s],
-            r.sem_ml_r.at[s],
-            head * share + (turn + s) % share,
-        )
-
-    def join(i):
-        peaks = [r.ml_own[i, 0:1, :]] + [r.ml_got[s, i, 0:1, :] for s in range(share - 1)]
-        peak = functools.reduce(jnp.maximum, peaks)
-        total = jnp.exp2((peaks[0] - peak) * LN2_SCALE) * r.ml_own[i, 1:2, :]
-        for s in range(share - 1):
-            weight = jnp.exp2((peaks[s + 1] - peak) * LN2_SCALE)
-            total = total + weight * r.ml_got[s, i, 1:2, :]
-        r.ml_own[i, 0:1, :] = peak
-        r.ml_own[i, 1:2, :] = 1.0 / total
-
-    def normal(n):
-        mine = p.own(n, turn)
-        first = p.offset(n, turn)
-
-        def one(i):
-            weight = jnp.exp2((r.ml[n * count + i, 0:1, :] - r.ml_own[i, 0:1, :]) * LN2_SCALE)
-            weight = weight * r.ml_own[i, 1:2, :]
-            e = r.cache[first + i - mine].astype(F32)
-            r.cache[first + i - mine] = (e * weight).astype(BF16)
-
-        loop(mine, count, one)
 
     def far_sum(g):
         rate = column(r.rate, g)
@@ -681,42 +678,38 @@
     hy_outs = (r.out_hq, r.out_hk, r.out_hv)
     give = [local(r.hy_out.at[i], hy_outs[i], r.sem_out.at[3 + i]) for i in range(3)]
 
-    for c in fetch_rest:
-        c.wait()
-    g_chunk(0)
-    arrive(0)
-    arrive(1)
+    arrive(0, 1)
     loop(1, heads, lambda d: in_copy(2, d, False).start())
+    loop(1, near, lambda d: near_copy(d, True).wait_recv())
+    r.st_got[my_near] = r.st_own[...]
+    loop(0, p.groups, near_sum)
+    loop(1, far, lambda d: far_copy(d).start())
     settle(0)
     settle(1)
-    g_arrive(0)
     loop(0, heads, turn_keys)
     loop(0, heads, spread)
     loop(0, count, combine)
     for s in range(1, share):
         ml_copy(s).start()
-    g_chunk(1)
+    for c in fetch_rest:
+        c.wait()
+    last = p.chunks - 1
+    g_chunks(0, last)
     fetch_o.wait()
     delta_half(0)
+    arrive(2)
     for s in range(1, share):
         ml_copy(s).wait_recv()
         ml_copy(s).wait_send()
     loop(0, count, join)
     loop(0, heads, normal)
-    g_arrive(1)
+    g_chunks(last, p.chunks)
+    delta_half(1)
+    settle(2)
+    for n in range(last):
+        g_arrive(n)
     delta_arrive(0)
-    loop(1, far, lambda d: far_copy(d).wait_recv())
-    loop(0, p.groups, far_sum)
-    g_chunk(2)
-    loop(0, p.groups, mix)
-    for c in give:
-        c.start()
-    arrive(2)
-    g_arrive(2)
-    settle(2)
-    g_chunk(3)
-    delta_half(1)
-    g_arrive(3)
+    g_arrive(last)
     delta_arrive(1)
     for s in range(1, share):
         for n in range(p.chunks):
@@ -813,7 +806,7 @@
                 grad_prob = dot_nt(r.v_seq[keys, :], r.g_seq[rows_at(i + u, tok), :])
                 change = grad_prob - r.delta_row[i + u, 0:1, :]
                 score = (r.cache[first + i + u].astype(F32) * change).astype(BF16)
-                r.dq_turn[i + u] += dot_nn(r.k_turn[n], score)
+                r.cache[first + i + u] = score
                 scores.append(score)
             queries = r.q_seq[pl.ds(pl.multiple_of(i * tok, tok), width * tok), :]
             return acc + dot_nn(jnp.concatenate(scores, axis=1), queries)
@@ -822,13 +815,24 @@
         keep(1, n, r.dk_seq, (acc * SCALE).astype(BF16))
 
     loop(0, heads, score_pass)
-
-    def turn_queries(i):
-        value = r.dq_turn[i].T * SCALE
+    kv_arrive(1, r.dk_seq)
+    hand_back(1, lambda place, h, b: r.dk_seq[place])
+
+    def query_pass(i):
+        def some(n, width, acc):
+            turned, scores = [], []
+            for u in range(width):
+                turned.append(r.k_turn[n + u])
+                scores.append(r.cache[p.offset(n + u, turn) + i - p.own(n + u, turn)])
+            left, right = jnp.concatenate(turned, axis=1), jnp.concatenate(scores, axis=0)
+            return acc + dot_nn(left, right)
+
+        acc = spans(0, p.held(i, turn), some, jnp.zeros((HD, tok), F32))
+        value = acc.T * SCALE
         r.dq_seq[2 * i] = value[:half]
         r.dq_seq[2 * i + 1] = value[half:]
 
-    loop(0, count, turn_queries)
+    loop(0, count, query_pass)
 
     def q_copy(s):
         return remote(
@@ -843,23 +847,27 @@
 
         def pick(f, s=s):
             place = place_of((turn + s) % share * heads * 2 + f)
-            r.dq_out[s - 1, f] = r.dq_seq[place]
+            r.dq_out[s - 1, f] = r.dq_seq[place].astype(BF16)
 
         loop(0, 2 * heads, pick)
         q_copy(s).start()
 
-    kv_arrive(1, r.dk_seq)
-    hand_back(1, lambda place, h, b: r.dk_seq[place])
+    loop(1, far, lambda d: far_copy(d).wait_recv())
+    loop(0, p.groups, far_sum)
+    loop(0, p.groups // 2, mix)
     for s in range(1, share):
         q_copy(s).wait_recv()
 
     def dq_value(place, h, b):
         value = r.dq_seq[place]
         for s in range(1, share):
-            value = value + r.dq_got[s - 1, 2 * h + b]
+            value = value + r.dq_got[s - 1, 2 * h + b].astype(F32)
         return value.astype(BF16)
 
     hand_back(0, dq_value)
+    loop(p.groups // 2, p.groups, mix)
+    for c in give:
+        c.start()
 
     for n in range(p.chunks):
         for d in range(1, p.parts):
@@ -869,7 +877,7 @@
     for i in range(3):
         loop(1, heads, lambda d, i=i: in_copy(i, d, False).wait_send())
         for s in range(1, share):
-            hand_on(alls[i], i, s, False, fw).wait_send()
+            loop(0, heads, lambda d, i=i, s=s: hand_on(i, d, s, False).wait_send())
     for n in range(p.chunks):
         loop(1, heads, lambda d, n=n: g_copy(n, d, False).wait_send())
     for b in range(2):

time: 153 us -> 118 us (0.77)
  Pallas kernels: 152 us -> 116 us
    pallas_call x1, Pallas kernels: 147 us -> 112 us  [body(): pl.pallas_call(functools.partial(kernel, p, names), in_specs=[pl.BlockSpe...]
where the time goes in v2:
time: 118 us; the launch traced here: 117 us
  Pallas kernels  116 us (98%)
    pallas_call x1, Pallas kernels, body(): pl.pallas_call(functools.partial(kernel, p, names), in_specs=[pl.BlockSpe...  112 us
    pallas_call x1, Pallas kernels, body(): pl.pallas_call(copy_kernel, in_specs=[hbm] * 6, out_specs=[hbm] * 6, out_...  4.43 us

profile of v2, /device:TPU:13, one launch (start us, length us, event | category | flops | bytes accessed | tf_op | source)
XLA Modules:
  0.0 116.7 jit_solution(79501356087340825)
XLA Ops:
  0.6 111.6 %grads.1 = (bf16[2,128,1024]{2,1,0:T(8,128)(2,1)}, bf16[2,128,1024]{2,1,0:T(8,128)(2,1)}, bf16[2,128,1024]{2,1,0:T(8,128)(2,1)}, bf16[256,2048]{1,0:T(8,128)(2,1...) custom-call(s32[32]{0:T(128)} %refs_0_.1, f32[16,16]{1,0:T(8,128)} %refs_1_.1, f32[16,16]{1,0:T(8,128)} %refs_2_.1, ...), custom_call_target="tpu_custom_call" | custom-call | tf_op jit(solution)/shard_map/grads/pallas_call | solution.py:953
  112.3 4.4 %results.1 = (bf16[2,128,1024]{2,1,0:T(8,128)(2,1)}, bf16[2,128,1024]{2,1,0:T(8,128)(2,1)}, bf16[2,128,1024]{2,1,0:T(8,128)(2,1)}, bf16[256,2048]{1,0:T(8,128)(2...) custom-call(bf16[2,128,1024]{2,1,0:T(8,128)(2,1)} %get-tuple-element.18.refs_0_, ...), custom_call_target="tpu_custom_call" | custom-call | tf_op jit(solution)/shard_map/results/pallas_call | solution.py:978

commit v3 on v2

--- a/solution.py
+++ b/solution.py
@@ -483,7 +483,8 @@
             high, low = split(prod)
             r.delta_out[b, h] = dot_nt(ones, high) + dot_nt(ones, low)
 
-        loop(0, heads, one)
+        for h in range(heads):
+            one(h)
         loop(1, heads, lambda d: delta_copy(b, d, False).start())
         r.delta_all[b * count + turn * heads + head] = r.delta_out[b, head]
 
@@ -680,10 +681,6 @@
 
     arrive(0, 1)
     loop(1, heads, lambda d: in_copy(2, d, False).start())
-    loop(1, near, lambda d: near_copy(d, True).wait_recv())
-    r.st_got[my_near] = r.st_own[...]
-    loop(0, p.groups, near_sum)
-    loop(1, far, lambda d: far_copy(d).start())
     settle(0)
     settle(1)
     loop(0, heads, turn_keys)
@@ -705,6 +702,10 @@
     loop(0, heads, normal)
     g_chunks(last, p.chunks)
     delta_half(1)
+    loop(1, near, lambda d: near_copy(d, True).wait_recv())
+    r.st_got[my_near] = r.st_own[...]
+    loop(0, p.groups, near_sum)
+    loop(1, far, lambda d: far_copy(d).start())
     settle(2)
     for n in range(last):
         g_arrive(n)
@@ -818,21 +819,30 @@
     kv_arrive(1, r.dk_seq)
     hand_back(1, lambda place, h, b: r.dk_seq[place])
 
-    def query_pass(i):
-        def some(n, width, acc):
-            turned, scores = [], []
-            for u in range(width):
-                turned.append(r.k_turn[n + u])
-                scores.append(r.cache[p.offset(n + u, turn) + i - p.own(n + u, turn)])
-            left, right = jnp.concatenate(turned, axis=1), jnp.concatenate(scores, axis=0)
-            return acc + dot_nn(left, right)
-
-        acc = spans(0, p.held(i, turn), some, jnp.zeros((HD, tok), F32))
-        value = acc.T * SCALE
-        r.dq_seq[2 * i] = value[:half]
-        r.dq_seq[2 * i + 1] = value[half:]
-
-    loop(0, count, query_pass)
+    def query_pass(t):
+        pair = (2 * t, 2 * t + 1)
+        both = p.held(pair[0], turn)
+
+        def some(n, width, accs, queries=pair):
+            spots = [p.offset(n + u, turn) - p.own(n + u, turn) for u in range(width)]
+            left = jnp.concatenate([r.k_turn[n + u] for u in range(width)], axis=1)
+            out = []
+            for acc, i in zip(accs, queries, strict=True):
+                right = jnp.concatenate([r.cache[spot + i] for spot in spots], axis=0)
+                out.append(acc + dot_nn(left, right))
+            return tuple(out)
+
+        zero = jnp.zeros((HD, tok), F32)
+        one, two = spans(0, both, some, (zero, zero))
+        (two,) = lax.fori_loop(
+            both, p.held(pair[1], turn), lambda n, c: some(n, 1, c, pair[1:]), (two,)
+        )
+        for i, acc in zip(pair, (one, two), strict=True):
+            value = acc.T * SCALE
+            r.dq_seq[2 * i] = value[:half]
+            r.dq_seq[2 * i + 1] = value[half:]
+
+    loop(0, count // 2, query_pass)
 
     def q_copy(s):
         return remote(
@@ -854,7 +864,7 @@
 
     loop(1, far, lambda d: far_copy(d).wait_recv())
     loop(0, p.groups, far_sum)
-    loop(0, p.groups // 2, mix)
+    loop(0, p.groups // 4, mix)
     for s in range(1, share):
         q_copy(s).wait_recv()
 
@@ -865,7 +875,7 @@
         return value.astype(BF16)
 
     hand_back(0, dq_value)
-    loop(p.groups // 2, p.groups, mix)
+    loop(p.groups // 4, p.groups, mix)
     for c in give:
         c.start()
 

time: 118 us -> 115 us (0.975)
  Pallas kernels: 116 us -> 113 us
    pallas_call x1, Pallas kernels: 112 us -> 108 us  [body(): pl.pallas_call(functools.partial(kernel, p, names), in_specs=[pl.BlockSpe...]
where the time goes in v3:
time: 115 us; the launch traced here: 113 us
  Pallas kernels  113 us (98%)
    pallas_call x1, Pallas kernels, body(): pl.pallas_call(functools.partial(kernel, p, names), in_specs=[pl.BlockSpe...  108 us
    pallas_call x1, Pallas kernels, body(): pl.pallas_call(copy_kernel, in_specs=[hbm] * 6, out_specs=[hbm] * 6, out_...  4.43 us

profile of v3, /device:TPU:13, one launch (start us, length us, event | category | flops | bytes accessed | tf_op | source)
XLA Modules:
  0.0 113.4 jit_solution(7286969025803758199)
XLA Ops:
  0.6 108.3 %grads.1 = (bf16[2,128,1024]{2,1,0:T(8,128)(2,1)}, bf16[2,128,1024]{2,1,0:T(8,128)(2,1)}, bf16[2,128,1024]{2,1,0:T(8,128)(2,1)}, bf16[256,2048]{1,0:T(8,128)(2,1...) custom-call(s32[32]{0:T(128)} %refs_0_.1, f32[16,16]{1,0:T(8,128)} %refs_1_.1, f32[16,16]{1,0:T(8,128)} %refs_2_.1, ...), custom_call_target="tpu_custom_call" | custom-call | tf_op jit(solution)/shard_map/grads/pallas_call | solution.py:963
  108.9 4.4 %results.1 = (bf16[2,128,1024]{2,1,0:T(8,128)(2,1)}, bf16[2,128,1024]{2,1,0:T(8,128)(2,1)}, bf16[2,128,1024]{2,1,0:T(8,128)(2,1)}, bf16[256,2048]{1,0:T(8,128)(2...) custom-call(bf16[2,128,1024]{2,1,0:T(8,128)(2,1)} %get-tuple-element.18.refs_0_, ...), custom_call_target="tpu_custom_call" | custom-call | tf_op jit(solution)/shard_map/results/pallas_call | solution.py:988
